TPU v7x, 256 devices: a whole 4x4x8 slice. The times are simulated.
256 devices in a mesh: seq: 32 (over x, z), vocab: 8 (over y, core).
Axes of the slice: x: 4, y: 4, z: 8, core: 2. Of those that a mesh axis runs over, the one named last changes fastest.
Arguments:
- hidden: bfloat16 [32768, 3584], P('seq', 'vocab'), may hold values from -6 to 6
- norm_gain: float32 [3584], replicated, may hold values from 0.25 to 1.75
- head_weight: bfloat16 [3584, 8000], P(None, 'vocab'), may hold values from -0.3125 to 0.3125
- teacher_ids: int32 [32768, 128], P('seq'), may hold values from 0 to 7999
- teacher_probs: float32 [32768, 128], P('seq'), may hold values from 0.0001 to 0.015
- doc_ids: int32 [32768], P('seq'), may hold values from -1 to 127, as said below
- plan: int32 [256, 2], P('seq'), may hold values from -1 to 31, as said below
Outputs:
- doc_loss: float32 [128], replicated
- row_lse: float32 [16384], P('seq')
Inputs may be any that keep to these rules, and one draw needn't show every extreme that they name: `plan`: row b of a seq index's 8 rows describes its home block b: a destination seq index and an owned slot 0 to 3 there, or -1 and -1 for a block without tokens. Live blocks of a seq index come first. Every owned slot of every seq index receives exactly one block, no seq index sends more than 1 block to one destination, and some seq index sends exactly 1 to some destination. `doc_ids`: -1 exactly on the rows of blocks without tokens. Over the live rows, taken seq index by seq index and in order, document numbers never fall; a document may be empty.
All inputs are finite; a program needn't handle non-finite values.
Results may differ from a plain program's by a relative error of at most 0.00035.
Values may be sent and summed in bfloat16 or wider, within the bound.
No kernel may reach another device: no remote copies, remote signals or barrier semaphores. Data moves between devices by JAX's collectives and lax.ppermute only.
A program may use at most 64 MiB of HBM per device.

v0:
```python
import functools

import jax
import jax.numpy as jnp
from jax import lax
from jax.experimental import pallas as pl
from jax.experimental.pallas import tpu as pltpu
from jax.sharding import PartitionSpec as P


BLOCK = 128
WORK = 4
DOCS = 128
CHIPS = 4
CORES = 2
CHUNKS = 2
HOPS = (0, 1, 3, 2)
SOFTCAP = 30.0
EPS = 1e-06
LANES = 128
MIB = 1 << 20


def on_diagonal():
    lane = lax.broadcasted_iota(jnp.int32, (BLOCK, LANES), 1)
    return lane == lax.broadcasted_iota(jnp.int32, (BLOCK, LANES), 0)


def as_row(column):
    return jnp.sum(jnp.where(on_diagonal(), column, 0.0), axis=0, keepdims=True)


def prepare_kernel(where_ref, weight_ref, gain_ref, out_ref, *scratch):
    parts, sems = scratch[:-1], scratch[-1]
    width = parts[0].shape[1]
    tiles = width // LANES
    chips = [lax.rem(where_ref[0] + hop, CHIPS) for hop in HOPS]
    copies = []
    for k, chip in enumerate(chips):
        start = pl.multiple_of(chip * width, LANES)
        copies.append(
            pltpu.make_async_copy(weight_ref.at[:, pl.ds(start, width)], parts[k], sems.at[k])
        )
        copies[k].start()
    for k, chip in enumerate(chips):
        copies[k].wait()
        for t in range(tiles):
            gain = gain_ref[pl.ds(chip * tiles + t, 1), :]
            part = parts[k][:, t * LANES : (t + 1) * LANES].astype(jnp.float32) * gain
            to = k * width + t * LANES
            out_ref[:, to : to + LANES] = part.astype(jnp.bfloat16)


def prepare(where, weight, gain):
    vmem = pl.BlockSpec(memory_space=pltpu.VMEM)
    vocab, features = weight.shape
    return pl.pallas_call(
        prepare_kernel,
        out_shape=jax.ShapeDtypeStruct(weight.shape, jnp.bfloat16),
        in_specs=[
            pl.BlockSpec(memory_space=pltpu.SMEM),
            pl.BlockSpec(memory_space=pltpu.HBM),
            vmem,
        ],
        out_specs=vmem,
        scratch_shapes=[pltpu.VMEM((vocab, features // CHIPS), jnp.bfloat16)] * CHIPS
        + [pltpu.SemaphoreType.DMA((CHIPS,))],
        compiler_params=pltpu.CompilerParams(vmem_limit_bytes=24 * MIB),
        cost_estimate=pl.CostEstimate(
            flops=500 * weight.size, bytes_accessed=4 * weight.size, transcendentals=0
        ),
        name="prepare",
    )(where, weight, gain)


def stack(core, pieces, rows_ref):
    shard, width = pieces[0].shape
    squares = jnp.zeros((16, width), jnp.float32)
    for k, piece in enumerate(pieces):
        pair, side = k // CORES, k % CORES
        start = pair * CORES * shard + (core if side == 0 else 1 - core) * shard

        def step(i, carry):
            at = pl.multiple_of(i * 16, 16)
            part = piece[pl.ds(at, 16), :]
            rows_ref[pl.ds(pl.multiple_of(start + at, 16), 16), :] = part
            wide = part.astype(jnp.float32)
            return carry + wide * wide

        squares = lax.fori_loop(0, shard // 16, step, squares, unroll=4)
    return squares


def near_kernel(where_ref, weight_ref, *refs):
    pieces, (logits_ref, squares_ref, rows_ref) = refs[:-3], refs[-3:]
    squares_ref[...] = stack(where_ref[1], pieces, rows_ref)
    logits_ref[...] = jnp.dot(
        weight_ref[:, : rows_ref.shape[0]], rows_ref[...], preferred_element_type=jnp.float32
    )


def near_head(where, weight, pieces):
    vocab, _ = weight.shape
    shard, width = pieces[0].shape
    depth = shard * len(pieces)
    vmem = pl.BlockSpec(memory_space=pltpu.VMEM)
    return pl.pallas_call(
        near_kernel,
        out_shape=(
            jax.ShapeDtypeStruct((vocab, width), jnp.float32),
            jax.ShapeDtypeStruct((16, width), jnp.float32),
        ),
        in_specs=[pl.BlockSpec(memory_space=pltpu.SMEM)] + [vmem] * (1 + len(pieces)),
        out_specs=(vmem, vmem),
        scratch_shapes=[pltpu.VMEM((depth, width), jnp.bfloat16)],
        compiler_params=pltpu.CompilerParams(vmem_limit_bytes=24 * MIB),
        cost_estimate=pl.CostEstimate(
            flops=2 * vocab * depth * width,
            bytes_accessed=2 * (vocab + width) * depth,
            transcendentals=0,
        ),
        name="near",
    )(where, weight, *pieces)


def far_kernel(chunk, features, count, where_ref, weight_ref, near_ref, squares_ref, ids_ref, probs_ref, *refs):
    pieces, refs = refs[:count], refs[count:]
    earlier = refs[0] if chunk else None
    outs, (rows_ref, logits_ref, scale_ref) = refs[bool(chunk) : -3], refs[-3:]
    vocab, depth = weight_ref.shape[0], rows_ref.shape[0]
    width = rows_ref.shape[1]
    squares = squares_ref[...] + stack(where_ref[1], pieces, rows_ref)
    mean = jnp.sum(squares, axis=0, keepdims=True) * (1.0 / features)
    scale = lax.rsqrt(mean + EPS) * (1.0 / SOFTCAP)
    scale_ref[...] = jnp.broadcast_to(scale, scale_ref.shape)
    logits_ref[...] = near_ref[...] + jnp.dot(
        weight_ref[:, features - depth :], rows_ref[...], preferred_element_type=jnp.float32
    )

    blocks = width // BLOCK
    expsums, picks = [], []
    for q in range(blocks):
        lanes = slice(q * BLOCK, (q + 1) * BLOCK)
        scale = scale_ref[0:1, lanes]
        rows = slice((chunk * blocks + q) * BLOCK, (chunk * blocks + q + 1) * BLOCK)
        within = ids_ref[rows, :] - where_ref[2]
        tile, spot = within >> 7, within & (LANES - 1)
        sums = jnp.zeros((8, BLOCK), jnp.float32)
        turned = []
        for t in range(-(-vocab // LANES)):
            size = min(LANES, vocab - t * LANES)
            soft = jnp.tanh(logits_ref[t * LANES : t * LANES + size, lanes] * scale)
            power = jnp.exp(SOFTCAP * soft)
            sums = sums + jnp.sum(power.reshape(size // 8, 8, BLOCK), axis=0)
            if size < LANES:
                soft = jnp.concatenate([soft, jnp.zeros((LANES - size, BLOCK), jnp.float32)], axis=0)
            turned.append(soft.T)
        chosen = []
        for g in range(0, BLOCK, 8):
            found = jnp.zeros((8, LANES), jnp.float32)
            for t, soft in enumerate(turned):
                part = jnp.take_along_axis(
                    soft[g : g + 8], spot[g : g + 8], axis=1, mode="promise_in_bounds"
                )
                found = jnp.where(tile[g : g + 8] == t, part, found)
            chosen.append(found)
        chosen = jnp.concatenate(chosen, axis=0)
        picked = SOFTCAP * jnp.sum(probs_ref[rows, :] * chosen, axis=1, keepdims=True)
        expsums.append(jnp.sum(sums, axis=0, keepdims=True))
        picks.append(as_row(picked))
    here = jnp.concatenate(expsums + picks, axis=0)
    if chunk == 0:
        stats_ref, mass_ref = outs
        stats_ref[...] = here
        for b in range(mass_ref.shape[0]):
            mass = jnp.sum(probs_ref[b * BLOCK : (b + 1) * BLOCK, :], axis=1, keepdims=True)
            mass_ref[b : b + 1, :] = as_row(mass)
    else:
        (copies_ref,) = outs
        before = earlier[...]
        for k in range(copies_ref.shape[0]):
            copies_ref[k, 0:blocks] = before[:blocks]
            copies_ref[k, blocks : 2 * blocks] = here[:blocks]
            copies_ref[k, 2 * blocks : 3 * blocks] = before[blocks:]
            copies_ref[k, 3 * blocks :] = here[blocks:]


def far_head(chunk, where, weight, near, squares, ids, probs, pieces, earlier, peers):
    vocab, features = weight.shape
    shard, width = pieces[0].shape[0], near.shape[1]
    blocks = ids.shape[0] // BLOCK
    stat = lambda *shape: jax.ShapeDtypeStruct(shape, jnp.float32)
    if chunk == 0:
        out_shape = (stat(blocks, BLOCK), stat(blocks, BLOCK))
    else:
        out_shape = (stat(peers, 2 * blocks, BLOCK),)
    vmem = pl.BlockSpec(memory_space=pltpu.VMEM)
    operands = [weight, near, squares, ids, probs, *pieces] + ([earlier] if chunk else [])
    depth = len(pieces) * shard
    return pl.pallas_call(
        functools.partial(far_kernel, chunk, features, len(pieces)),
        out_shape=out_shape,
        in_specs=[pl.BlockSpec(memory_space=pltpu.SMEM)] + [vmem] * len(operands),
        out_specs=(vmem,) * len(out_shape),
        scratch_shapes=[
            pltpu.VMEM((depth, width), jnp.bfloat16),
            pltpu.VMEM((vocab, width), jnp.float32),
            pltpu.VMEM((8, width), jnp.float32),
        ],
        compiler_params=pltpu.CompilerParams(vmem_limit_bytes=24 * MIB),
        cost_estimate=pl.CostEstimate(
            flops=2 * 2 * vocab * depth * width,
            bytes_accessed=2 * (vocab + width) * depth + 8 * vocab * width,
            transcendentals=2 * vocab * width,
        ),
        name="far",
    )(where, *operands)


def losses_kernel(plan_ref, came_ref, mass_ref, docs_ref, message_ref):
    blocks = mass_ref.shape[0]
    sums = jnp.sum(came_ref[...], axis=0)
    expsum, picked = sums[:blocks], sums[blocks:]
    alive = docs_ref[...] >= 0
    lse = jnp.log(jnp.where(alive, expsum, 1.0))
    row_loss = jnp.where(alive, lse * mass_ref[...] - picked, 0.0)
    label = lax.broadcasted_iota(jnp.int32, (DOCS, LANES), 0)
    totals = jnp.zeros((DOCS, LANES), jnp.float32)
    counts = jnp.zeros((DOCS, LANES), jnp.float32)
    for b in range(blocks):
        member = label == docs_ref[b : b + 1, :]
        totals = totals + jnp.where(member, row_loss[b : b + 1, :], 0.0)
        counts = counts + jnp.where(member, 1.0, 0.0)
    totals = as_row(jnp.sum(totals, axis=1, keepdims=True))
    counts = as_row(jnp.sum(counts, axis=1, keepdims=True))
    peers = message_ref.shape[0]
    peer = lax.broadcasted_iota(jnp.int32, (peers, LANES), 0)
    routed = jnp.zeros((peers, LANES), jnp.float32)
    mark = jnp.zeros((peers, LANES), jnp.int32)
    for b in range(blocks):
        chosen = peer == plan_ref[0, b]
        routed = jnp.where(chosen, lse[b : b + 1, :], routed)
        mark = jnp.where(chosen, plan_ref[1, b] + 1, mark)
    message_ref[:, 0 * LANES : 1 * LANES] = routed
    message_ref[:, 1 * LANES : 2 * LANES] = jnp.broadcast_to(totals, (peers, LANES))
    message_ref[:, 2 * LANES : 3 * LANES] = jnp.broadcast_to(counts, (peers, LANES))
    message_ref[:, 3 * LANES : 4 * LANES] = mark.astype(jnp.float32)


def losses(plan, came, mass, docs, peers):
    vmem = pl.BlockSpec(memory_space=pltpu.VMEM)
    return pl.pallas_call(
        losses_kernel,
        out_shape=jax.ShapeDtypeStruct((peers, 4 * LANES), jnp.float32),
        in_specs=[pl.BlockSpec(memory_space=pltpu.SMEM), vmem, vmem, vmem],
        out_specs=vmem,
        compiler_params=pltpu.CompilerParams(vmem_limit_bytes=8 * MIB),
        name="losses",
    )(plan, came, mass, docs)


def finish_kernel(came_ref, doc_ref, lse_ref):
    mark = came_ref[:, 3 * LANES : 4 * LANES]
    came = came_ref[:, 0:LANES]
    for s in range(WORK):
        lse_ref[s : s + 1, :] = jnp.sum(
            jnp.where(mark == float(s + 1), came, 0.0), axis=0, keepdims=True
        )
    totals = jnp.sum(came_ref[:, LANES : 2 * LANES], axis=0, keepdims=True)
    counts = jnp.sum(came_ref[:, 2 * LANES : 3 * LANES], axis=0, keepdims=True)
    doc_ref[...] = totals / jnp.maximum(counts, 1.0)


def finish(came):
    vmem = pl.BlockSpec(memory_space=pltpu.VMEM)
    stat = lambda rows: jax.ShapeDtypeStruct((rows, LANES), jnp.float32)
    return pl.pallas_call(
        finish_kernel,
        out_shape=(stat(1), stat(WORK)),
        in_specs=[vmem],
        out_specs=(vmem, vmem),
        compiler_params=pltpu.CompilerParams(vmem_limit_bytes=8 * MIB),
        name="finish",
    )(came)


def turn(step):
    count = CORES * CHIPS
    return [(i, (i + CORES * step) % count) for i in range(count)]


SWAP = [(i, i ^ 1) for i in range(CORES * CHIPS)]


def move(x, pairs):
    return lax.ppermute(x, "vocab", pairs)


def per_device(hidden, norm_gain, head_weight, teacher_ids, teacher_probs, doc_ids, plan):
    seq_count, peers = lax.axis_size("seq"), lax.axis_size("vocab")
    vocab_local = head_weight.shape[1]
    shard = lax.axis_index("vocab")
    where = jnp.stack([shard // CORES, shard % CORES, shard * vocab_local]).astype(jnp.int32)
    turned = hidden.T
    width = turned.shape[1] // CHUNKS
    first, second = turned[:, :width], turned[:, width:]
    a0 = move(first, turn(1))
    b1 = move(second, turn(-1))
    b0 = move(first, turn(-1))
    weight = prepare(where, head_weight.T, norm_gain.reshape(-1, LANES))
    c0 = move(a0, turn(1))
    a1 = move(second, turn(1))
    c1 = move(b1, turn(-1))
    z0, z1 = move(first, SWAP), move(second, SWAP)
    a0s, b1s, b0s = move(a0, SWAP), move(b1, SWAP), move(b0, SWAP)
    c0s, c1s, a1s = move(c0, SWAP), move(c1, SWAP), move(a1, SWAP)
    near1 = near_head(where, weight, (second, z1, b1, b1s))
    near0 = near_head(where, weight, (first, z0, b0, b0s, a0, a0s))
    teacher = (teacher_ids, teacher_probs)
    earlier, mass = far_head(0, where, weight, *near0, *teacher, (c0, c0s), None, peers)
    (copies,) = far_head(1, where, weight, *near1, *teacher, (a1, a1s, c1, c1s), earlier, peers)

    came = lax.all_to_all(copies, "vocab", split_axis=0, concat_axis=0, tiled=True)
    message = losses(plan.T, came, mass, doc_ids.reshape(-1, BLOCK), seq_count)
    came = lax.all_to_all(message, "seq", split_axis=0, concat_axis=0, tiled=True)
    doc_loss, row_lse = finish(came)
    return (doc_loss.reshape(-1), row_lse.reshape(-1))


def solution(mesh):
    return jax.shard_map(
        per_device,
        mesh=mesh,
        in_specs=(
            P("seq", "vocab"),
            P(),
            P(None, "vocab"),
            P("seq", None),
            P("seq", None),
            P("seq"),
            P("seq", None),
        ),
        out_specs=(P(), P("seq")),
        check_vma=False,
    )
```

profile of v0, /device:TPU:1, one launch (start us, length us, event | category | flops | bytes accessed | tf_op | source)
XLA Modules:
  0.0 94.0 jit_solution(7528429373548588684)
XLA Ops:
  0.6 1.2 %fusion = (bf16[448,512]{1,0:T(8,128)(2,1)S(1)}, bf16[448,512]{1,0:T(8,128)(2,1)S(1)}) fusion(bf16[448,1024]{1,0:T(8,128)(2,1)} %bitcast.20), kind=kLoop, calls=%fused_computation.2 | loop fusion | bytes 1835008 | tf_op jit(solution)/shard_map/slice | solution.py:306
  1.9 2.2 %collective-permute-start.10 = (bf16[448,512]{1,0:T(8,128)(2,1)S(1)}, bf16[448,512]{1,0:T(8,128)(2,1)S(1)}, u32[]{:S(2)}, u32[]{:S(2)}) collective-permute-start(bf16[448,512]{1,0:T(8,128)(2,1)S(1)} %get-tuple-element.18.refs_0_), channel_id=1, source_target_pairs={{0,2},{1,3},{2,4},{3,5},{4,6},{5,7},{6,0},{7,1},{8,10},{9,11},{10,... | collective-permute-start | bytes 1376264 | tf_op jit(solution)/shard_map/ppermute | solution.py:296
  4.0 1.5 %collective-permute-start.8 = (bf16[448,512]{1,0:T(8,128)(2,1)S(1)}, bf16[448,512]{1,0:T(8,128)(2,1)}, u32[]{:S(2)}, u32[]{:S(2)}) collective-permute-start(bf16[448,512]{1,0:T(8,128)(2,1)S(1)} %get-tuple-element.18.refs_0_), channel_id=1, source_target_pairs={{0,6},{1,7},{2,0},{3,1},{4,2},{5,3},{6,4},{7,5},{8,14},{9,15},{10,... | collective-permute-start | bytes 1376264 | tf_op jit(solution)/shard_map/ppermute | solution.py:296
  5.6 1.4 %collective-permute-start.1 = (bf16[448,512]{1,0:T(8,128)(2,1)S(1)}, bf16[448,512]{1,0:T(8,128)(2,1)S(1)}, u32[]{:S(2)}, u32[]{:S(2)}) collective-permute-start(bf16[448,512]{1,0:T(8,128)(2,1)S(1)} %get-tuple-element.19.refs_0_), channel_id=1, source_target_pairs={{0,6},{1,7},{2,0},{3,1},{4,2},{5,3},{6,4},{7,5},{8,14},{9,15},{10,... | collective-permute-start | bytes 1376264 | tf_op jit(solution)/shard_map/ppermute | solution.py:296
  6.9 1.5 %collective-permute-start.7 = (bf16[448,512]{1,0:T(8,128)(2,1)S(1)}, bf16[448,512]{1,0:T(8,128)(2,1)S(1)}, u32[]{:S(2)}, u32[]{:S(2)}) collective-permute-start(bf16[448,512]{1,0:T(8,128)(2,1)S(1)} %get-tuple-element.18.refs_0_), channel_id=1, source_target_pairs={{0,1},{1,0},{2,3},{3,2},{4,5},{5,4},{6,7},{7,6},{8,9},{9,8},{10,11... | collective-permute-start | bytes 1376264 | tf_op jit(solution)/shard_map/ppermute | solution.py:296
  8.5 0.0 collective-permute-start
  8.5 5.3 %collective-permute-done.10.refs_4_ = bf16[448,512]{1,0:T(8,128)(2,1)S(1)} collective-permute-done((bf16[448,512]{1,0:T(8,128)(2,1)S(1)}, bf16[448,512]{1,0:T(8,128)(2,1)S(1)}, u32[]{:S(2)}, u32[]{:S(2)}) %collective-permute-start.10) | collective-permute-done | bytes 458784 | tf_op jit(solution)/shard_map/ppermute | solution.py:296
  13.8 1.6 %collective-permute-start.3 = (bf16[448,512]{1,0:T(8,128)(2,1)S(1)}, bf16[448,512]{1,0:T(8,128)(2,1)S(1)}, u32[]{:S(2)}, u32[]{:S(2)}) collective-permute-start(bf16[448,512]{1,0:T(8,128)(2,1)S(1)} %get-tuple-element.19.refs_0_), channel_id=1, source_target_pairs={{0,2},{1,3},{2,4},{3,5},{4,6},{5,7},{6,0},{7,1},{8,10},{9,11},{10,... | collective-permute-start | bytes 1376264 | tf_op jit(solution)/shard_map/ppermute | solution.py:296
  15.4 0.0 collective-permute-done.8.refs_2_
  15.4 1.4 %collective-permute-start.12 = (bf16[448,512]{1,0:T(8,128)(2,1)S(1)}, bf16[448,512]{1,0:T(8,128)(2,1)S(1)}, u32[]{:S(2)}, u32[]{:S(2)}) collective-permute-start(bf16[448,512]{1,0:T(8,128)(2,1)S(1)} %collective-permute-done.10.refs_4_), channel_id=1, source_target_pairs={{0,2},{1,3},{2,4},{3,5},{4,6},{5,7},{6,0},{7,1},{8,10},{9,11},{10,... | collective-permute-start | bytes 1376264 | tf_op jit(solution)/shard_map/ppermute | solution.py:296
  16.9 7.9 %collective-permute-done.1.refs_2_ = bf16[448,512]{1,0:T(8,128)(2,1)S(1)} collective-permute-done((bf16[448,512]{1,0:T(8,128)(2,1)S(1)}, bf16[448,512]{1,0:T(8,128)(2,1)S(1)}, u32[]{:S(2)}, u32[]{:S(2)}) %collective-permute-start.1) | collective-permute-done | bytes 458784 | tf_op jit(solution)/shard_map/ppermute | solution.py:296
  24.8 2.0 %collective-permute-start.2 = (bf16[448,512]{1,0:T(8,128)(2,1)S(1)}, bf16[448,512]{1,0:T(8,128)(2,1)S(1)}, u32[]{:S(2)}, u32[]{:S(2)}) collective-permute-start(bf16[448,512]{1,0:T(8,128)(2,1)S(1)} %collective-permute-done.1.refs_2_), channel_id=1, source_target_pairs={{0,1},{1,0},{2,3},{3,2},{4,5},{5,4},{6,7},{7,6},{8,9},{9,8},{10,11... | collective-permute-start | bytes 1376264 | tf_op jit(solution)/shard_map/ppermute | solution.py:296
  26.8 0.0 collective-permute-done.7.refs_1_
  26.8 0.0 copy-start.8
  26.8 0.8 copy-done.8
  27.6 2.7 %collective-permute-start.5 = (bf16[448,512]{1,0:T(8,128)(2,1)S(1)}, bf16[448,512]{1,0:T(8,128)(2,1)}, u32[]{:S(2)}, u32[]{:S(2)}) collective-permute-start(bf16[448,512]{1,0:T(8,128)(2,1)S(1)} %collective-permute-done.1.refs_2_), channel_id=1, source_target_pairs={{0,6},{1,7},{2,0},{3,1},{4,2},{5,3},{6,4},{7,5},{8,14},{9,15},{10,... | collective-permute-start | bytes 1376264 | tf_op jit(solution)/shard_map/ppermute | solution.py:296
  30.3 0.0 collective-permute-done.refs_1_
  30.4 0.3 collective-permute-start.11
  30.6 0.0 collective-permute-done.3.refs_0_
  30.6 0.0 copy-start.6
  30.6 0.8 copy-done.6
  31.4 0.9 collective-permute-start.9
  32.3 0.1 pad_add_fusion.where_ref
  32.4 2.4 %collective-permute-done.12.refs_0_ = bf16[448,512]{1,0:T(8,128)(2,1)S(1)} collective-permute-done((bf16[448,512]{1,0:T(8,128)(2,1)S(1)}, bf16[448,512]{1,0:T(8,128)(2,1)S(1)}, u32[]{:S(2)}, u32[]{:S(2)}) %collective-permute-start.12) | collective-permute-done | bytes 458784 | tf_op jit(solution)/shard_map/ppermute | solution.py:296
  34.8 3.5 %collective-permute-start.13 = (bf16[448,512]{1,0:T(8,128)(2,1)S(1)}, bf16[448,512]{1,0:T(8,128)(2,1)S(1)}, u32[]{:S(2)}, u32[]{:S(2)}) collective-permute-start(bf16[448,512]{1,0:T(8,128)(2,1)S(1)} %collective-permute-done.12.refs_0_), channel_id=1, source_target_pairs={{0,1},{1,0},{2,3},{3,2},{4,5},{5,4},{6,7},{7,6},{8,9},{9,8},{10,11... | collective-permute-start | bytes 1376264 | tf_op jit(solution)/shard_map/ppermute | solution.py:296
  38.3 0.0 copy-start
  38.3 3.0 %copy-done = bf16[3584,1000]{0,1:T(8,128)(2,1)S(1)} copy-done((bf16[3584,1000]{0,1:T(8,128)(2,1)S(1)}, bf16[3584,1000]{0,1:T(8,128)(2,1)}, u32[]{:S(2)}) %copy-start) | copy-done | bytes 7168024
  41.3 0.0 copy-start.3
  41.3 0.7 copy-done.3
  42.1 0.0 copy-start.7
  42.1 2.6 %prepare.1.weight_ref = bf16[1000,3584]{1,0:T(8,128)(2,1)S(1)} custom-call(s32[3]{0:T(128)S(1)} %pad_add_fusion.where_ref, bf16[1000,3584]{1,0:T(8,128)(2,1)S(1)} %bitcast.14, f32[28,128]{1,0:T(8,128)S(1)} %bitcast.17), custom_call_target="tpu_custom_call" | custom-call | flops 1792000000 | bytes 14336000 | tf_op jit(solution)/shard_map/prepare/pallas_call | solution.py:57
  44.6 0.0 copy-start.9
  44.7 0.0 collective-permute-done.2.refs_3_
  44.7 0.0 copy-done.7
  44.7 0.1 collective-permute-start.4
  44.8 0.0 collective-permute-done.5.refs_2_
  44.8 0.5 collective-permute-start.6
  45.3 3.1 %near.2 = (f32[1000,512]{1,0:T(8,128)S(1)}, f32[16,512]{1,0:T(8,128)S(1)}) custom-call(s32[3]{0:T(128)S(1)} %pad_add_fusion.where_ref, bf16[1000,3584]{1,0:T(8,128)(2,1)S(1)} %prepare.1.weight_ref, bf16[448,512]{1,0:T(8,128)(2,1)S(1)} %get-tuple-element.19.refs_0_, bf16[448,512]{1,0:T(8,128)(2,1)S(1)} %collective-permute-done.refs_1_, ...), custom_call_target="tpu_custom_call" | custom-call | flops 1835008000 | bytes 5419008 | tf_op jit(solution)/shard_map/near/pallas_call | solution.py:107
  48.4 0.0 copy-start.1
  48.4 0.0 copy-start.2
  48.4 0.0 collective-permute-done.11.refs_5_
  48.4 0.0 collective-permute-done.9.refs_3_
  48.4 0.0 copy-done.9
  48.4 5.2 %near.3 = (f32[1000,512]{1,0:T(8,128)S(1)}, f32[16,512]{1,0:T(8,128)S(1)}) custom-call(s32[3]{0:T(128)S(1)} %pad_add_fusion.where_ref, bf16[1000,3584]{1,0:T(8,128)(2,1)S(1)} %prepare.1.weight_ref, bf16[448,512]{1,0:T(8,128)(2,1)S(1)} %get-tuple-element.18.refs_0_, bf16[448,512]{1,0:T(8,128)(2,1)S(1)} %copy-done.9, ...), custom_call_target="tpu_custom_call" | custom-call | flops 2752512000 | bytes 8128512 | tf_op jit(solution)/shard_map/near/pallas_call | solution.py:107
  53.6 0.0 collective-permute-done.13.refs_1_
  53.7 0.0 copy-done.1
  53.7 0.0 copy-done.2
  53.7 4.5 %far.2 = (f32[8,128]{1,0:T(8,128)S(1)}, f32[8,128]{1,0:T(8,128)S(1)}) custom-call(s32[3]{0:T(128)S(1)} %pad_add_fusion.where_ref, bf16[1000,3584]{1,0:T(8,128)(2,1)S(1)} %prepare.1.weight_ref, f32[1000,512]{1,0:T(8,128)S(1)} %get-tuple-element.12.near_ref, f32[16,512]{1,0:T(8,128)S(1)} %get-tuple-element.13.squares_ref, s32[1024,128]{1,0:T(8,128)S(1)} %copy-done.1, ...), custom_call_target="tpu_custom_call" | custom-call | flops 1835008000 | bytes 6805504 | tf_op jit(solution)/shard_map/far/pallas_call | solution.py:200
  58.2 0.0 copy-start.4
  58.2 0.0 copy-start.5
  58.2 0.0 collective-permute-done.4.refs_1_
  58.3 0.0 collective-permute-done.6.refs_3_
  58.3 5.9 %far.3 = f32[8,16,128]{2,1,0:T(8,128)S(1)} custom-call(s32[3]{0:T(128)S(1)} %pad_add_fusion.where_ref, bf16[1000,3584]{1,0:T(8,128)(2,1)S(1)} %prepare.1.weight_ref, f32[1000,512]{1,0:T(8,128)S(1)} %get-tuple-element.10.near_ref, f32[16,512]{1,0:T(8,128)S(1)} %get-tuple-element.11.squares_ref, s32[1024,128]{1,0:T(8,128)S(1)} %copy-done.1, ...), custom_call_target="tpu_custom_call" | custom-call | flops 3670016000 | bytes 9515008 | tf_op jit(solution)/shard_map/far/pallas_call | solution.py:200
  64.2 8.1 %all_to_all.16.came_ref = f32[8,16,128]{2,1,0:T(8,128)S(1)} all-to-all(f32[8,16,128]{2,1,0:T(8,128)S(1)} %far.3), channel_id=1, replica_groups=mesh['seq'=32,'vocab'=8] {'vocab'}, dimensions={0} | all-to-all | bytes 131072 | tf_op jit(solution)/shard_map/all_to_all | solution.py:323
  72.3 0.0 copy-done.4
  72.3 0.0 copy-done.5
  72.3 0.8 losses.1
  73.1 0.1 copy.9
  73.2 20.2 %all_to_all.17 = f32[32,1,512]{2,1,0:T(1,128)S(1)} all-to-all(f32[32,1,512]{2,1,0:T(1,128)S(1)} %copy.9), channel_id=1, replica_groups=mesh['seq'=32,'vocab'=8] {'seq'}, dimensions={0} | all-to-all | bytes 131072 | tf_op jit(solution)/shard_map/all_to_all | solution.py:325
  93.4 0.6 finish.1
  (1 shorter events, 0.0 us)
Async XLA Ops:
  1.9 11.9 %collective-permute-start.10 = (bf16[448,512]{1,0:T(8,128)(2,1)S(1)}, bf16[448,512]{1,0:T(8,128)(2,1)S(1)}, u32[]{:S(2)}, u32[]{:S(2)}) collective-permute-start(bf16[448,512]{1,0:T(8,128)(2,1)S(1)} %get-tuple-element.18.refs_0_), channel_id=1, source_target_pairs={{0,2},{1,3},{2,4},{3,5},{4,6},{5,7},{6,0},{7,1},{8,10},{9,11},{10,... | collective-permute-start | bytes 1376264 | tf_op jit(solution)/shard_map/ppermute | solution.py:296
  4.0 11.4 %collective-permute-start.8 = (bf16[448,512]{1,0:T(8,128)(2,1)S(1)}, bf16[448,512]{1,0:T(8,128)(2,1)}, u32[]{:S(2)}, u32[]{:S(2)}) collective-permute-start(bf16[448,512]{1,0:T(8,128)(2,1)S(1)} %get-tuple-element.18.refs_0_), channel_id=1, source_target_pairs={{0,6},{1,7},{2,0},{3,1},{4,2},{5,3},{6,4},{7,5},{8,14},{9,15},{10,... | collective-permute-start | bytes 1376264 | tf_op jit(solution)/shard_map/ppermute | solution.py:296
  5.6 19.2 %collective-permute-start.1 = (bf16[448,512]{1,0:T(8,128)(2,1)S(1)}, bf16[448,512]{1,0:T(8,128)(2,1)S(1)}, u32[]{:S(2)}, u32[]{:S(2)}) collective-permute-start(bf16[448,512]{1,0:T(8,128)(2,1)S(1)} %get-tuple-element.19.refs_0_), channel_id=1, source_target_pairs={{0,6},{1,7},{2,0},{3,1},{4,2},{5,3},{6,4},{7,5},{8,14},{9,15},{10,... | collective-permute-start | bytes 1376264 | tf_op jit(solution)/shard_map/ppermute | solution.py:296
  6.9 19.9 %collective-permute-start.7 = (bf16[448,512]{1,0:T(8,128)(2,1)S(1)}, bf16[448,512]{1,0:T(8,128)(2,1)S(1)}, u32[]{:S(2)}, u32[]{:S(2)}) collective-permute-start(bf16[448,512]{1,0:T(8,128)(2,1)S(1)} %get-tuple-element.18.refs_0_), channel_id=1, source_target_pairs={{0,1},{1,0},{2,3},{3,2},{4,5},{5,4},{6,7},{7,6},{8,9},{9,8},{10,11... | collective-permute-start | bytes 1376264 | tf_op jit(solution)/shard_map/ppermute | solution.py:296
  8.5 21.9 %collective-permute-start = (bf16[448,512]{1,0:T(8,128)(2,1)S(1)}, bf16[448,512]{1,0:T(8,128)(2,1)S(1)}, u32[]{:S(2)}, u32[]{:S(2)}) collective-permute-start(bf16[448,512]{1,0:T(8,128)(2,1)S(1)} %get-tuple-element.19.refs_0_), channel_id=1, source_target_pairs={{0,1},{1,0},{2,3},{3,2},{4,5},{5,4},{6,7},{7,6},{8,9},{9,8},{10,11... | collective-permute-start | bytes 1376264 | tf_op jit(solution)/shard_map/ppermute | solution.py:296
  13.8 16.9 %collective-permute-start.3 = (bf16[448,512]{1,0:T(8,128)(2,1)S(1)}, bf16[448,512]{1,0:T(8,128)(2,1)S(1)}, u32[]{:S(2)}, u32[]{:S(2)}) collective-permute-start(bf16[448,512]{1,0:T(8,128)(2,1)S(1)} %get-tuple-element.19.refs_0_), channel_id=1, source_target_pairs={{0,2},{1,3},{2,4},{3,5},{4,6},{5,7},{6,0},{7,1},{8,10},{9,11},{10,... | collective-permute-start | bytes 1376264 | tf_op jit(solution)/shard_map/ppermute | solution.py:296
  15.4 19.4 %collective-permute-start.12 = (bf16[448,512]{1,0:T(8,128)(2,1)S(1)}, bf16[448,512]{1,0:T(8,128)(2,1)S(1)}, u32[]{:S(2)}, u32[]{:S(2)}) collective-permute-start(bf16[448,512]{1,0:T(8,128)(2,1)S(1)} %collective-permute-done.10.refs_4_), channel_id=1, source_target_pairs={{0,2},{1,3},{2,4},{3,5},{4,6},{5,7},{6,0},{7,1},{8,10},{9,11},{10,... | collective-permute-start | bytes 1376264 | tf_op jit(solution)/shard_map/ppermute | solution.py:296
  24.8 19.9 %collective-permute-start.2 = (bf16[448,512]{1,0:T(8,128)(2,1)S(1)}, bf16[448,512]{1,0:T(8,128)(2,1)S(1)}, u32[]{:S(2)}, u32[]{:S(2)}) collective-permute-start(bf16[448,512]{1,0:T(8,128)(2,1)S(1)} %collective-permute-done.1.refs_2_), channel_id=1, source_target_pairs={{0,1},{1,0},{2,3},{3,2},{4,5},{5,4},{6,7},{7,6},{8,9},{9,8},{10,11... | collective-permute-start | bytes 1376264 | tf_op jit(solution)/shard_map/ppermute | solution.py:296
  26.8 0.8 copy-start.8
  27.6 17.2 %collective-permute-start.5 = (bf16[448,512]{1,0:T(8,128)(2,1)S(1)}, bf16[448,512]{1,0:T(8,128)(2,1)}, u32[]{:S(2)}, u32[]{:S(2)}) collective-permute-start(bf16[448,512]{1,0:T(8,128)(2,1)S(1)} %collective-permute-done.1.refs_2_), channel_id=1, source_target_pairs={{0,6},{1,7},{2,0},{3,1},{4,2},{5,3},{6,4},{7,5},{8,14},{9,15},{10,... | collective-permute-start | bytes 1376264 | tf_op jit(solution)/shard_map/ppermute | solution.py:296
  30.4 18.0 %collective-permute-start.11 = (bf16[448,512]{1,0:T(8,128)(2,1)S(1)}, bf16[448,512]{1,0:T(8,128)(2,1)}, u32[]{:S(2)}, u32[]{:S(2)}) collective-permute-start(bf16[448,512]{1,0:T(8,128)(2,1)S(1)} %collective-permute-done.10.refs_4_), channel_id=1, source_target_pairs={{0,1},{1,0},{2,3},{3,2},{4,5},{5,4},{6,7},{7,6},{8,9},{9,8},{10,11... | collective-permute-start | bytes 1376264 | tf_op jit(solution)/shard_map/ppermute | solution.py:296
  30.6 0.8 copy-start.6
  31.4 17.0 %collective-permute-start.9 = (bf16[448,512]{1,0:T(8,128)(2,1)}, bf16[448,512]{1,0:T(8,128)(2,1)}, u32[]{:S(2)}, u32[]{:S(2)}) collective-permute-start(bf16[448,512]{1,0:T(8,128)(2,1)} %collective-permute-done.8.refs_2_), channel_id=1, source_target_pairs={{0,1},{1,0},{2,3},{3,2},{4,5},{5,4},{6,7},{7,6},{8,9},{9,8},{10,11... | collective-permute-start | bytes 1376264 | tf_op jit(solution)/shard_map/ppermute | solution.py:296
  34.8 18.9 %collective-permute-start.13 = (bf16[448,512]{1,0:T(8,128)(2,1)S(1)}, bf16[448,512]{1,0:T(8,128)(2,1)S(1)}, u32[]{:S(2)}, u32[]{:S(2)}) collective-permute-start(bf16[448,512]{1,0:T(8,128)(2,1)S(1)} %collective-permute-done.12.refs_0_), channel_id=1, source_target_pairs={{0,1},{1,0},{2,3},{3,2},{4,5},{5,4},{6,7},{7,6},{8,9},{9,8},{10,11... | collective-permute-start | bytes 1376264 | tf_op jit(solution)/shard_map/ppermute | solution.py:296
  38.3 3.1 %copy-start = (bf16[3584,1000]{0,1:T(8,128)(2,1)S(1)}, bf16[3584,1000]{0,1:T(8,128)(2,1)}, u32[]{:S(2)}) copy-start(bf16[3584,1000]{0,1:T(8,128)(2,1)} %param.9) | copy-start | bytes 21504004
  41.3 0.7 copy-start.3
  42.1 2.6 %copy-start.7 = (bf16[448,512]{1,0:T(8,128)(2,1)S(1)}, bf16[448,512]{1,0:T(8,128)(2,1)}, u32[]{:S(2)}) copy-start(bf16[448,512]{1,0:T(8,128)(2,1)} %copy-done.6) | copy-start | bytes 1376260
  44.6 3.8 %copy-start.9 = (bf16[448,512]{1,0:T(8,128)(2,1)S(1)}, bf16[448,512]{1,0:T(8,128)(2,1)}, u32[]{:S(2)}) copy-start(bf16[448,512]{1,0:T(8,128)(2,1)} %copy-done.8) | copy-start | bytes 1376260
  44.7 13.6 %collective-permute-start.4 = (bf16[448,512]{1,0:T(8,128)(2,1)S(1)}, bf16[448,512]{1,0:T(8,128)(2,1)S(1)}, u32[]{:S(2)}, u32[]{:S(2)}) collective-permute-start(bf16[448,512]{1,0:T(8,128)(2,1)S(1)} %copy-done.7), channel_id=1, source_target_pairs={{0,1},{1,0},{2,3},{3,2},{4,5},{5,4},{6,7},{7,6},{8,9},{9,8},{10,11... | collective-permute-start | bytes 1376264 | tf_op jit(solution)/shard_map/ppermute | solution.py:296
  44.8 13.5 %collective-permute-start.6 = (bf16[448,512]{1,0:T(8,128)(2,1)}, bf16[448,512]{1,0:T(8,128)(2,1)S(1)}, u32[]{:S(2)}, u32[]{:S(2)}) collective-permute-start(bf16[448,512]{1,0:T(8,128)(2,1)} %collective-permute-done.5.refs_2_), channel_id=1, source_target_pairs={{0,1},{1,0},{2,3},{3,2},{4,5},{5,4},{6,7},{7,6},{8,9},{9,8},{10,11... | collective-permute-start | bytes 1376264 | tf_op jit(solution)/shard_map/ppermute | solution.py:296
  48.4 5.3 %copy-start.1 = (s32[1024,128]{1,0:T(8,128)S(1)}, s32[1024,128]{1,0:T(8,128)}, u32[]{:S(2)}) copy-start(s32[1024,128]{1,0:T(8,128)} %ids_ref.3) | copy-start | bytes 1572868
  48.4 5.3 %copy-start.2 = (f32[1024,128]{1,0:T(8,128)S(1)}, f32[1024,128]{1,0:T(8,128)}, u32[]{:S(2)}) copy-start(f32[1024,128]{1,0:T(8,128)} %probs_ref.3) | copy-start | bytes 1572868
  58.2 14.1 %copy-start.4 = (s32[1024]{0:T(1024)S(1)}, s32[1024]{0:T(1024)}, u32[]{:S(2)}) copy-start(s32[1024]{0:T(1024)} %param.12) | copy-start | bytes 12292
  58.2 14.1 %copy-start.5 = (s32[8,2]{0,1:T(2,128)S(1)}, s32[8,2]{0,1:T(2,128)}, u32[]{:S(2)}) copy-start(s32[8,2]{0,1:T(2,128)} %param.13) | copy-start | bytes 196
where the time goes:
time: 94.3 us; the launch traced here: 94 us
  blocking collectives  28.4 us (30%)
  Pallas kernels  22.7 us (24%)
  starting transfers between devices  19.7 us (21%)
  waiting for transfers between devices  15.6 us (17%)
  local copies, waits for them, and re-layouts  6.68 us (7%)
    all_to_all x1, blocking collectives, per_device(): lax.all_to_all(message, 'seq', split_axis=0, concat_axis=0, tiled=True)  20.2 us
    ppermute x14, starting transfers between devices, move(): return lax.ppermute(x, 'vocab', pairs)  19.7 us
    ppermute x14, waiting for transfers between devices, move(): return lax.ppermute(x, 'vocab', pairs)  15.6 us
    pallas_call x2, Pallas kernels, far_head(): pl.pallas_call(functools.partial(far_kernel, chunk, features, len(pieces)...  10.4 us
    pallas_call x2, Pallas kernels, near_head(): pl.pallas_call(near_kernel, out_shape=(jax.ShapeDtypeStruct((vocab, width...  8.3 us
    all_to_all x1, blocking collectives, per_device(): lax.all_to_all(copies, 'vocab', split_axis=0, concat_axis=0, tiled=True)  8.13 us
    unnamed x21, local copies, waits for them, and re-layouts  5.39 us
    pallas_call x1, Pallas kernels, prepare(): pl.pallas_call(prepare_kernel, out_shape=jax.ShapeDtypeStruct(weight.shap...  2.58 us
  transfers between devices with their start and end apart: 14, of which 3 were waited for; matrix products, arithmetic and copies ran while one was open for 0% of the time, Pallas kernels for 16%

commit v1 on v0

--- a/solution.py
+++ b/solution.py
@@ -14,7 +14,7 @@
 CHIPS = 4
 CORES = 2
 CHUNKS = 2
-HOPS = (0, 1, 3, 2)
+HOPS = (1, 0, 3, 2, 1)
 SOFTCAP = 30.0
 EPS = 1e-06
 LANES = 128
@@ -30,23 +30,23 @@
     return jnp.sum(jnp.where(on_diagonal(), column, 0.0), axis=0, keepdims=True)
 
 
-def prepare_kernel(where_ref, weight_ref, gain_ref, out_ref, *scratch):
-    parts, sems = scratch[:-1], scratch[-1]
-    width = parts[0].shape[1]
+def prepare_kernel(where_ref, weight_ref, gain_ref, out_ref):
+    width = weight_ref.shape[1] // CHIPS
     tiles = width // LANES
-    chips = [lax.rem(where_ref[0] + hop, CHIPS) for hop in HOPS]
-    copies = []
-    for k, chip in enumerate(chips):
-        start = pl.multiple_of(chip * width, LANES)
-        copies.append(
-            pltpu.make_async_copy(weight_ref.at[:, pl.ds(start, width)], parts[k], sems.at[k])
-        )
-        copies[k].start()
-    for k, chip in enumerate(chips):
-        copies[k].wait()
+    low = lax.broadcasted_iota(jnp.int32, (1, LANES), 1) < width // CORES % LANES
+    for k, hop in enumerate(HOPS):
+        chips = [lax.rem(where_ref[0] + h, CHIPS) for h in (hop, (CHIPS - hop) % CHIPS)]
         for t in range(tiles):
-            gain = gain_ref[pl.ds(chip * tiles + t, 1), :]
-            part = parts[k][:, t * LANES : (t + 1) * LANES].astype(jnp.float32) * gain
+
+            def scaled(chip):
+                gain = gain_ref[pl.ds(chip * tiles + t, 1), :]
+                start = pl.multiple_of(chip * width + t * LANES, LANES)
+                return weight_ref[:, pl.ds(start, LANES)].astype(jnp.float32) * gain
+
+            if t == tiles // 2:
+                part = jnp.where(low, scaled(chips[0]), scaled(chips[1]))
+            else:
+                part = scaled(chips[t > tiles // 2])
             to = k * width + t * LANES
             out_ref[:, to : to + LANES] = part.astype(jnp.bfloat16)
 
@@ -56,15 +56,9 @@
     vocab, features = weight.shape
     return pl.pallas_call(
         prepare_kernel,
-        out_shape=jax.ShapeDtypeStruct(weight.shape, jnp.bfloat16),
-        in_specs=[
-            pl.BlockSpec(memory_space=pltpu.SMEM),
-            pl.BlockSpec(memory_space=pltpu.HBM),
-            vmem,
-        ],
+        out_shape=jax.ShapeDtypeStruct((vocab, features // CHIPS * len(HOPS)), jnp.bfloat16),
+        in_specs=[pl.BlockSpec(memory_space=pltpu.SMEM), vmem, vmem],
         out_specs=vmem,
-        scratch_shapes=[pltpu.VMEM((vocab, features // CHIPS), jnp.bfloat16)] * CHIPS
-        + [pltpu.SemaphoreType.DMA((CHIPS,))],
         compiler_params=pltpu.CompilerParams(vmem_limit_bytes=24 * MIB),
         cost_estimate=pl.CostEstimate(
             flops=500 * weight.size, bytes_accessed=4 * weight.size, transcendentals=0
@@ -73,46 +67,53 @@
     )(where, weight, gain)
 
 
-def stack(core, pieces, rows_ref):
-    shard, width = pieces[0].shape
-    squares = jnp.zeros((16, width), jnp.float32)
-    for k, piece in enumerate(pieces):
-        pair, side = k // CORES, k % CORES
-        start = pair * CORES * shard + (core if side == 0 else 1 - core) * shard
-
-        def step(i, carry):
-            at = pl.multiple_of(i * 16, 16)
-            part = piece[pl.ds(at, 16), :]
-            rows_ref[pl.ds(pl.multiple_of(start + at, 16), 16), :] = part
-            wide = part.astype(jnp.float32)
-            return carry + wide * wide
-
-        squares = lax.fori_loop(0, shard // 16, step, squares, unroll=4)
-    return squares
-
-
-def near_kernel(where_ref, weight_ref, *refs):
-    pieces, (logits_ref, squares_ref, rows_ref) = refs[:-3], refs[-3:]
-    squares_ref[...] = stack(where_ref[1], pieces, rows_ref)
-    logits_ref[...] = jnp.dot(
-        weight_ref[:, : rows_ref.shape[0]], rows_ref[...], preferred_element_type=jnp.float32
+def squares_of(pieces):
+    total = 0.0
+    for piece in pieces:
+        for i in range(0, piece[0].shape[0], 16):
+            wide = across(piece, i, 16).astype(jnp.float32)
+            total = total + wide * wide
+    return total
+
+
+def across(piece, start, count):
+    parts = [part[start : start + count, :] for part in piece]
+    return parts[0] if len(parts) == 1 else jnp.concatenate(parts, axis=1)
+
+
+def multiply(core, weight_ref, first, pieces):
+    shard = pieces[0][0].shape[0]
+    start, depth = first * CORES * shard, len(pieces) * shard
+    rows = []
+    for own, other in zip(pieces[::CORES], pieces[1::CORES]):
+        own, other = across(own, 0, shard), across(other, 0, shard)
+        rows += [jnp.where(core == 0, own, other), jnp.where(core == 0, other, own)]
+    return jnp.dot(
+        weight_ref[:, start : start + depth],
+        jnp.concatenate(rows, axis=0),
+        preferred_element_type=jnp.float32,
     )
 
 
-def near_head(where, weight, pieces):
-    vocab, _ = weight.shape
+def near_kernel(first, where_ref, weight_ref, *refs):
+    pieces, (logits_ref, squares_ref) = [(p,) for p in refs[:-2]], refs[-2:]
+    squares_ref[...] = squares_of(pieces)
+    logits_ref[...] = multiply(where_ref[1], weight_ref, first, pieces)
+
+
+def near_head(first, where, weight, pieces):
+    vocab = weight.shape[0]
     shard, width = pieces[0].shape
     depth = shard * len(pieces)
     vmem = pl.BlockSpec(memory_space=pltpu.VMEM)
     return pl.pallas_call(
-        near_kernel,
+        functools.partial(near_kernel, first),
         out_shape=(
             jax.ShapeDtypeStruct((vocab, width), jnp.float32),
             jax.ShapeDtypeStruct((16, width), jnp.float32),
         ),
         in_specs=[pl.BlockSpec(memory_space=pltpu.SMEM)] + [vmem] * (1 + len(pieces)),
         out_specs=(vmem, vmem),
-        scratch_shapes=[pltpu.VMEM((depth, width), jnp.bfloat16)],
         compiler_params=pltpu.CompilerParams(vmem_limit_bytes=24 * MIB),
         cost_estimate=pl.CostEstimate(
             flops=2 * vocab * depth * width,
@@ -123,19 +124,19 @@
     )(where, weight, *pieces)
 
 
-def far_kernel(chunk, features, count, where_ref, weight_ref, near_ref, squares_ref, ids_ref, probs_ref, *refs):
-    pieces, refs = refs[:count], refs[count:]
+def far_kernel(chunk, first, features, counts, where_ref, weight_ref, near_ref, squares_ref, ids_ref, probs_ref, *refs):
+    pieces = []
+    for count in counts:
+        pieces.append(refs[:count])
+        refs = refs[count:]
     earlier = refs[0] if chunk else None
-    outs, (rows_ref, logits_ref, scale_ref) = refs[bool(chunk) : -3], refs[-3:]
-    vocab, depth = weight_ref.shape[0], rows_ref.shape[0]
-    width = rows_ref.shape[1]
-    squares = squares_ref[...] + stack(where_ref[1], pieces, rows_ref)
+    outs, (logits_ref, scale_ref) = refs[bool(chunk) : -2], refs[-2:]
+    vocab, width = near_ref.shape
+    squares = squares_ref[...] + squares_of(pieces)
     mean = jnp.sum(squares, axis=0, keepdims=True) * (1.0 / features)
     scale = lax.rsqrt(mean + EPS) * (1.0 / SOFTCAP)
     scale_ref[...] = jnp.broadcast_to(scale, scale_ref.shape)
-    logits_ref[...] = near_ref[...] + jnp.dot(
-        weight_ref[:, features - depth :], rows_ref[...], preferred_element_type=jnp.float32
-    )
+    logits_ref[...] = near_ref[...] + multiply(where_ref[1], weight_ref, first, pieces)
 
     blocks = width // BLOCK
     expsums, picks = [], []
@@ -154,7 +155,7 @@
             sums = sums + jnp.sum(power.reshape(size // 8, 8, BLOCK), axis=0)
             if size < LANES:
                 soft = jnp.concatenate([soft, jnp.zeros((LANES - size, BLOCK), jnp.float32)], axis=0)
-            turned.append(soft.T)
+            turned.append(soft.astype(jnp.bfloat16).T.astype(jnp.float32))
         chosen = []
         for g in range(0, BLOCK, 8):
             found = jnp.zeros((8, LANES), jnp.float32)
@@ -185,9 +186,11 @@
             copies_ref[k, 3 * blocks :] = here[blocks:]
 
 
-def far_head(chunk, where, weight, near, squares, ids, probs, pieces, earlier, peers):
-    vocab, features = weight.shape
-    shard, width = pieces[0].shape[0], near.shape[1]
+def far_head(chunk, first, where, weight, near, squares, ids, probs, pieces, earlier, peers):
+    vocab, width = near.shape
+    counts = [len(piece) for piece in pieces]
+    shard = pieces[0][0].shape[0]
+    features = shard * CORES * CHIPS
     blocks = ids.shape[0] // BLOCK
     stat = lambda *shape: jax.ShapeDtypeStruct(shape, jnp.float32)
     if chunk == 0:
@@ -195,15 +198,15 @@
     else:
         out_shape = (stat(peers, 2 * blocks, BLOCK),)
     vmem = pl.BlockSpec(memory_space=pltpu.VMEM)
-    operands = [weight, near, squares, ids, probs, *pieces] + ([earlier] if chunk else [])
+    parts = [part for piece in pieces for part in piece]
+    operands = [weight, near, squares, ids, probs, *parts] + ([earlier] if chunk else [])
     depth = len(pieces) * shard
     return pl.pallas_call(
-        functools.partial(far_kernel, chunk, features, len(pieces)),
+        functools.partial(far_kernel, chunk, first, features, counts),
         out_shape=out_shape,
         in_specs=[pl.BlockSpec(memory_space=pltpu.SMEM)] + [vmem] * len(operands),
         out_specs=(vmem,) * len(out_shape),
         scratch_shapes=[
-            pltpu.VMEM((depth, width), jnp.bfloat16),
             pltpu.VMEM((vocab, width), jnp.float32),
             pltpu.VMEM((8, width), jnp.float32),
         ],
@@ -285,8 +288,11 @@
 
 
 def turn(step):
-    count = CORES * CHIPS
-    return [(i, (i + CORES * step) % count) for i in range(count)]
+    pairs = []
+    for i in range(CORES * CHIPS):
+        chip, core = i // CORES, i % CORES
+        pairs.append((i, (chip + (step if core == 0 else -step)) % CHIPS * CORES + core))
+    return pairs
 
 
 SWAP = [(i, i ^ 1) for i in range(CORES * CHIPS)]
@@ -314,11 +320,16 @@
     z0, z1 = move(first, SWAP), move(second, SWAP)
     a0s, b1s, b0s = move(a0, SWAP), move(b1, SWAP), move(b0, SWAP)
     c0s, c1s, a1s = move(c0, SWAP), move(c1, SWAP), move(a1, SWAP)
-    near1 = near_head(where, weight, (second, z1, b1, b1s))
-    near0 = near_head(where, weight, (first, z0, b0, b0s, a0, a0s))
+    near1 = near_head(0, where, weight, (b1, b1s, second, z1))
+    near0 = near_head(1, where, weight, (first, z0, a0, a0s))
     teacher = (teacher_ids, teacher_probs)
-    earlier, mass = far_head(0, where, weight, *near0, *teacher, (c0, c0s), None, peers)
-    (copies,) = far_head(1, where, weight, *near1, *teacher, (a1, a1s, c1, c1s), earlier, peers)
+    earlier, mass = far_head(
+        0, 3, where, weight, *near0, *teacher, ((c0,), (c0s,), (b0,), (b0s,)), None, peers
+    )
+    late = ((a1,), (a1s,), (c1,), (c1s,))
+    (copies,) = far_head(
+        1, 2, where, weight, *near1, *teacher, late, earlier, peers
+    )
 
     came = lax.all_to_all(copies, "vocab", split_axis=0, concat_axis=0, tiled=True)
     message = losses(plan.T, came, mass, doc_ids.reshape(-1, BLOCK), seq_count)

time: 94.3 us -> 80.8 us (0.86)
  Pallas kernels: 22.7 us -> 18.5 us
  starting transfers between devices: 19.7 us -> 15.6 us
  blocking collectives: 28.4 us -> 24.3 us
    pallas_call x5, Pallas kernels: 21.3 us -> 17.1 us  [the longest x2 8.41 us: far_head(): pl.pallas_call(functools.partial(far_kernel, chunk, first, features, coun...]
    ppermute x14, starting transfers between devices: 19.7 us -> 15.6 us  [move(): return lax.ppermute(x, 'vocab', pairs)]
    all_to_all x1, blocking collectives: 20.2 us -> 16.9 us  [per_device(): lax.all_to_all(message, 'seq', split_axis=0, concat_axis=0, tiled=True)]
    unnamed x21 -> x17, local copies, waits for them, and re-layouts: 5.39 us -> 4.59 us
where the time goes in v1:
time: 80.8 us; the launch traced here: 80.5 us
  blocking collectives  24.3 us (30%)
  Pallas kernels  18.5 us (23%)
  starting transfers between devices  15.6 us (19%)
  waiting for transfers between devices  15.3 us (19%)
  local copies, waits for them, and re-layouts  5.88 us (7%)
    all_to_all x1, blocking collectives, per_device(): lax.all_to_all(message, 'seq', split_axis=0, concat_axis=0, tiled=True)  16.9 us
    ppermute x14, starting transfers between devices, move(): return lax.ppermute(x, 'vocab', pairs)  15.6 us
    ppermute x14, waiting for transfers between devices, move(): return lax.ppermute(x, 'vocab', pairs)  15.3 us
    pallas_call x2, Pallas kernels, far_head(): pl.pallas_call(functools.partial(far_kernel, chunk, first, features, coun...  8.41 us
    all_to_all x1, blocking collectives, per_device(): lax.all_to_all(copies, 'vocab', split_axis=0, concat_axis=0, tiled=True)  7.44 us
    pallas_call x2, Pallas kernels, near_head(): pl.pallas_call(functools.partial(near_kernel, first), out_shape=(jax.Shap...  6.3 us
    unnamed x17, local copies, waits for them, and re-layouts  4.59 us
    pallas_call x1, Pallas kernels, prepare(): pl.pallas_call(prepare_kernel, out_shape=jax.ShapeDtypeStruct((vocab, fea...  2.43 us
  transfers between devices with their start and end apart: 14, of which 3 were waited for; matrix products, arithmetic and copies ran while one was open for 0% of the time, Pallas kernels for 16%

profile of v1, /device:TPU:1, one launch (start us, length us, event | category | flops | bytes accessed | tf_op | source)
XLA Modules:
  0.0 80.5 jit_solution(8060894328969118251)
XLA Ops:
  0.6 1.2 %fusion = (bf16[448,512]{1,0:T(8,128)(2,1)S(1)}, bf16[448,512]{1,0:T(8,128)(2,1)S(1)}) fusion(bf16[448,1024]{1,0:T(8,128)(2,1)} %bitcast.20), kind=kLoop, calls=%fused_computation.2 | loop fusion | bytes 1835008 | tf_op jit(solution)/shard_map/slice | solution.py:312
  1.9 3.6 %collective-permute-start.8 = (bf16[448,512]{1,0:T(8,128)(2,1)S(1)}, bf16[448,512]{1,0:T(8,128)(2,1)}, u32[]{:S(2)}, u32[]{:S(2)}) collective-permute-start(bf16[448,512]{1,0:T(8,128)(2,1)S(1)} %get-tuple-element.18.refs_0_), channel_id=1, source_target_pairs={{0,2},{1,7},{2,4},{3,1},{4,6},{5,3},{6,0},{7,5},{8,10},{9,15},{10,... | collective-permute-start | bytes 1376264 | tf_op jit(solution)/shard_map/ppermute | solution.py:302
  5.5 0.0 collective-permute-start.7
  5.5 0.8 %collective-permute-start.12 = (bf16[448,512]{1,0:T(8,128)(2,1)S(1)}, bf16[448,512]{1,0:T(8,128)(2,1)S(1)}, u32[]{:S(2)}, u32[]{:S(2)}) collective-permute-start(bf16[448,512]{1,0:T(8,128)(2,1)S(1)} %get-tuple-element.18.refs_0_), channel_id=1, source_target_pairs={{0,6},{1,3},{2,0},{3,5},{4,2},{5,7},{6,4},{7,1},{8,14},{9,11},{10,... | collective-permute-start | bytes 1376264 | tf_op jit(solution)/shard_map/ppermute | solution.py:302
  6.3 1.0 %collective-permute-start = (bf16[448,512]{1,0:T(8,128)(2,1)S(1)}, bf16[448,512]{1,0:T(8,128)(2,1)S(1)}, u32[]{:S(2)}, u32[]{:S(2)}) collective-permute-start(bf16[448,512]{1,0:T(8,128)(2,1)S(1)} %get-tuple-element.19.refs_2_), channel_id=1, source_target_pairs={{0,6},{1,3},{2,0},{3,5},{4,2},{5,7},{6,4},{7,1},{8,14},{9,11},{10,... | collective-permute-start | bytes 1376264 | tf_op jit(solution)/shard_map/ppermute | solution.py:302
  7.3 1.2 %collective-permute-start.2 = (bf16[448,512]{1,0:T(8,128)(2,1)S(1)}, bf16[448,512]{1,0:T(8,128)(2,1)S(1)}, u32[]{:S(2)}, u32[]{:S(2)}) collective-permute-start(bf16[448,512]{1,0:T(8,128)(2,1)S(1)} %get-tuple-element.19.refs_2_), channel_id=1, source_target_pairs={{0,1},{1,0},{2,3},{3,2},{4,5},{5,4},{6,7},{7,6},{8,9},{9,8},{10,11... | collective-permute-start | bytes 1376264 | tf_op jit(solution)/shard_map/ppermute | solution.py:302
  8.5 4.3 %collective-permute-done.8.refs_2_ = bf16[448,512]{1,0:T(8,128)(2,1)} collective-permute-done((bf16[448,512]{1,0:T(8,128)(2,1)S(1)}, bf16[448,512]{1,0:T(8,128)(2,1)}, u32[]{:S(2)}, u32[]{:S(2)}) %collective-permute-start.8) | collective-permute-done | bytes 458784 | tf_op jit(solution)/shard_map/ppermute | solution.py:302
  12.7 7.1 %collective-permute-start.9 = (bf16[448,512]{1,0:T(8,128)(2,1)}, bf16[448,512]{1,0:T(8,128)(2,1)}, u32[]{:S(2)}, u32[]{:S(2)}) collective-permute-start(bf16[448,512]{1,0:T(8,128)(2,1)} %collective-permute-done.8.refs_2_), channel_id=1, source_target_pairs={{0,1},{1,0},{2,3},{3,2},{4,5},{5,4},{6,7},{7,6},{8,9},{9,8},{10,11... | collective-permute-start | bytes 1376264 | tf_op jit(solution)/shard_map/ppermute | solution.py:302
  19.8 0.0 collective-permute-done.7.refs_1_
  19.8 0.0 copy-start.3
  19.8 0.8 copy-done.3
  20.6 0.0 collective-permute-start.10
  20.6 0.0 collective-permute-done.12.refs_2_
  20.6 0.0 collective-permute-start.3
  20.6 3.2 %collective-permute-done.refs_0_ = bf16[448,512]{1,0:T(8,128)(2,1)S(1)} collective-permute-done((bf16[448,512]{1,0:T(8,128)(2,1)S(1)}, bf16[448,512]{1,0:T(8,128)(2,1)S(1)}, u32[]{:S(2)}, u32[]{:S(2)}) %collective-permute-start) | collective-permute-done | bytes 458784 | tf_op jit(solution)/shard_map/ppermute | solution.py:302
  23.9 0.0 collective-permute-start.5
  23.9 0.0 collective-permute-done.2.refs_3_
  23.9 1.0 %collective-permute-start.1 = (bf16[448,512]{1,0:T(8,128)(2,1)S(1)}, bf16[448,512]{1,0:T(8,128)(2,1)}, u32[]{:S(2)}, u32[]{:S(2)}) collective-permute-start(bf16[448,512]{1,0:T(8,128)(2,1)S(1)} %collective-permute-done.refs_0_), channel_id=1, source_target_pairs={{0,1},{1,0},{2,3},{3,2},{4,5},{5,4},{6,7},{7,6},{8,9},{9,8},{10,11... | collective-permute-start | bytes 1376264 | tf_op jit(solution)/shard_map/ppermute | solution.py:302
  24.8 0.1 pad_add_fusion.where_ref
  24.9 0.0 collective-permute-done.9.refs_3_
  24.9 0.0 collective-permute-start.13
  24.9 7.8 %collective-permute-done.10.refs_0_ = bf16[448,512]{1,0:T(8,128)(2,1)S(1)} collective-permute-done((bf16[448,512]{1,0:T(8,128)(2,1)}, bf16[448,512]{1,0:T(8,128)(2,1)S(1)}, u32[]{:S(2)}, u32[]{:S(2)}) %collective-permute-start.10) | collective-permute-done | bytes 458784 | tf_op jit(solution)/shard_map/ppermute | solution.py:302
  32.7 0.2 collective-permute-start.11
  32.9 0.0 copy-start
  32.9 3.0 %copy-done = bf16[3584,1000]{0,1:T(8,128)(2,1)S(1)} copy-done((bf16[3584,1000]{0,1:T(8,128)(2,1)S(1)}, bf16[3584,1000]{0,1:T(8,128)(2,1)}, u32[]{:S(2)}) %copy-start) | copy-done | bytes 7168024
  36.0 0.0 copy-start.5
  36.0 0.7 copy-done.5
  36.7 0.0 copy-start.4
  36.7 2.4 %prepare.1.weight_ref = bf16[1000,4480]{1,0:T(8,128)(2,1)S(1)} custom-call(s32[3]{0:T(128)S(1)} %pad_add_fusion.where_ref, bf16[1000,3584]{1,0:T(8,128)(2,1)S(1)} %bitcast.14, f32[28,128]{1,0:T(8,128)S(1)} %bitcast.17), custom_call_target="tpu_custom_call" | custom-call | flops 1792000000 | bytes 14336000 | tf_op jit(solution)/shard_map/prepare/pallas_call | solution.py:57
  39.1 0.0 copy-done.4
  39.1 3.2 %near.3 = (f32[1000,512]{1,0:T(8,128)S(1)}, f32[16,512]{1,0:T(8,128)S(1)}) custom-call(s32[3]{0:T(128)S(1)} %pad_add_fusion.where_ref, bf16[1000,4480]{1,0:T(8,128)(2,1)S(1)} %prepare.1.weight_ref, bf16[448,512]{1,0:T(8,128)(2,1)S(1)} %get-tuple-element.18.refs_0_, bf16[448,512]{1,0:T(8,128)(2,1)S(1)} %copy-done.4, ...), custom_call_target="tpu_custom_call" | custom-call | flops 1835008000 | bytes 5419008 | tf_op jit(solution)/shard_map/near/pallas_call | solution.py:109
  42.3 0.0 copy-start.1
  42.4 0.0 copy-start.2
  42.4 0.0 collective-permute-done.3.refs_0_
  42.4 0.4 collective-permute-start.4
  42.8 0.0 collective-permute-done.5.refs_2_
  42.8 0.3 collective-permute-start.6
  43.1 0.0 collective-permute-done.1.refs_1_
  43.1 3.1 %near.2 = (f32[1000,512]{1,0:T(8,128)S(1)}, f32[16,512]{1,0:T(8,128)S(1)}) custom-call(s32[3]{0:T(128)S(1)} %pad_add_fusion.where_ref, bf16[1000,4480]{1,0:T(8,128)(2,1)S(1)} %prepare.1.weight_ref, bf16[448,512]{1,0:T(8,128)(2,1)S(1)} %collective-permute-done.refs_0_, bf16[448,512]{1,0:T(8,128)(2,1)} %collective-permute-done.1.refs_1_, ...), custom_call_target="tpu_custom_call" | custom-call | flops 1835008000 | bytes 5419008 | tf_op jit(solution)/shard_map/near/pallas_call | solution.py:109
  46.2 0.0 collective-permute-done.13.refs_3_
  46.2 0.0 collective-permute-done.11.refs_1_
  46.2 0.0 copy-done.1
  46.2 0.0 copy-done.2
  46.2 4.0 %far.2 = (f32[8,128]{1,0:T(8,128)S(1)}, f32[8,128]{1,0:T(8,128)S(1)}) custom-call(s32[3]{0:T(128)S(1)} %pad_add_fusion.where_ref, bf16[1000,4480]{1,0:T(8,128)(2,1)S(1)} %prepare.1.weight_ref, f32[1000,512]{1,0:T(8,128)S(1)} %get-tuple-element.12.near_ref, f32[16,512]{1,0:T(8,128)S(1)} %get-tuple-element.13.squares_ref, s32[1024,128]{1,0:T(8,128)S(1)} %copy-done.1, ...), custom_call_target="tpu_custom_call" | custom-call | flops 3670016000 | bytes 9515008 | tf_op jit(solution)/shard_map/far/pallas_call | solution.py:204
  50.2 0.0 copy-start.6
  50.2 0.0 copy-start.7
  50.2 0.0 collective-permute-done.4.refs_1_
  50.3 0.0 collective-permute-done.6.refs_3_
  50.3 4.4 %far.3 = f32[8,16,128]{2,1,0:T(8,128)S(1)} custom-call(s32[3]{0:T(128)S(1)} %pad_add_fusion.where_ref, bf16[1000,4480]{1,0:T(8,128)(2,1)S(1)} %prepare.1.weight_ref, f32[1000,512]{1,0:T(8,128)S(1)} %get-tuple-element.10.near_ref, f32[16,512]{1,0:T(8,128)S(1)} %get-tuple-element.11.squares_ref, s32[1024,128]{1,0:T(8,128)S(1)} %copy-done.1, ...), custom_call_target="tpu_custom_call" | custom-call | flops 3670016000 | bytes 9515008 | tf_op jit(solution)/shard_map/far/pallas_call | solution.py:204
  54.7 7.4 %all_to_all.16.came_ref = f32[8,16,128]{2,1,0:T(8,128)S(1)} all-to-all(f32[8,16,128]{2,1,0:T(8,128)S(1)} %far.3), channel_id=1, replica_groups=mesh['seq'=32,'vocab'=8] {'vocab'}, dimensions={0} | all-to-all | bytes 131072 | tf_op jit(solution)/shard_map/all_to_all | solution.py:334
  62.1 0.0 copy-done.6
  62.1 0.0 copy-done.7
  62.1 0.8 losses.1
  62.9 0.1 copy.9
  63.0 16.9 %all_to_all.17 = f32[32,1,512]{2,1,0:T(1,128)S(1)} all-to-all(f32[32,1,512]{2,1,0:T(1,128)S(1)} %copy.9), channel_id=1, replica_groups=mesh['seq'=32,'vocab'=8] {'seq'}, dimensions={0} | all-to-all | bytes 131072 | tf_op jit(solution)/shard_map/all_to_all | solution.py:336
  79.9 0.6 finish.1
  (1 shorter events, 0.0 us)
Async XLA Ops:
  1.9 10.9 %collective-permute-start.8 = (bf16[448,512]{1,0:T(8,128)(2,1)S(1)}, bf16[448,512]{1,0:T(8,128)(2,1)}, u32[]{:S(2)}, u32[]{:S(2)}) collective-permute-start(bf16[448,512]{1,0:T(8,128)(2,1)S(1)} %get-tuple-element.18.refs_0_), channel_id=1, source_target_pairs={{0,2},{1,7},{2,4},{3,1},{4,6},{5,3},{6,0},{7,5},{8,10},{9,15},{10,... | collective-permute-start | bytes 1376264 | tf_op jit(solution)/shard_map/ppermute | solution.py:302
  5.5 14.4 %collective-permute-start.7 = (bf16[448,512]{1,0:T(8,128)(2,1)S(1)}, bf16[448,512]{1,0:T(8,128)(2,1)S(1)}, u32[]{:S(2)}, u32[]{:S(2)}) collective-permute-start(bf16[448,512]{1,0:T(8,128)(2,1)S(1)} %get-tuple-element.18.refs_0_), channel_id=1, source_target_pairs={{0,1},{1,0},{2,3},{3,2},{4,5},{5,4},{6,7},{7,6},{8,9},{9,8},{10,11... | collective-permute-start | bytes 1376264 | tf_op jit(solution)/shard_map/ppermute | solution.py:302
  5.5 15.2 %collective-permute-start.12 = (bf16[448,512]{1,0:T(8,128)(2,1)S(1)}, bf16[448,512]{1,0:T(8,128)(2,1)S(1)}, u32[]{:S(2)}, u32[]{:S(2)}) collective-permute-start(bf16[448,512]{1,0:T(8,128)(2,1)S(1)} %get-tuple-element.18.refs_0_), channel_id=1, source_target_pairs={{0,6},{1,3},{2,0},{3,5},{4,2},{5,7},{6,4},{7,1},{8,14},{9,11},{10,... | collective-permute-start | bytes 1376264 | tf_op jit(solution)/shard_map/ppermute | solution.py:302
  6.3 17.6 %collective-permute-start = (bf16[448,512]{1,0:T(8,128)(2,1)S(1)}, bf16[448,512]{1,0:T(8,128)(2,1)S(1)}, u32[]{:S(2)}, u32[]{:S(2)}) collective-permute-start(bf16[448,512]{1,0:T(8,128)(2,1)S(1)} %get-tuple-element.19.refs_2_), channel_id=1, source_target_pairs={{0,6},{1,3},{2,0},{3,5},{4,2},{5,7},{6,4},{7,1},{8,14},{9,11},{10,... | collective-permute-start | bytes 1376264 | tf_op jit(solution)/shard_map/ppermute | solution.py:302
  7.3 16.6 %collective-permute-start.2 = (bf16[448,512]{1,0:T(8,128)(2,1)S(1)}, bf16[448,512]{1,0:T(8,128)(2,1)S(1)}, u32[]{:S(2)}, u32[]{:S(2)}) collective-permute-start(bf16[448,512]{1,0:T(8,128)(2,1)S(1)} %get-tuple-element.19.refs_2_), channel_id=1, source_target_pairs={{0,1},{1,0},{2,3},{3,2},{4,5},{5,4},{6,7},{7,6},{8,9},{9,8},{10,11... | collective-permute-start | bytes 1376264 | tf_op jit(solution)/shard_map/ppermute | solution.py:302
  12.7 12.2 %collective-permute-start.9 = (bf16[448,512]{1,0:T(8,128)(2,1)}, bf16[448,512]{1,0:T(8,128)(2,1)}, u32[]{:S(2)}, u32[]{:S(2)}) collective-permute-start(bf16[448,512]{1,0:T(8,128)(2,1)} %collective-permute-done.8.refs_2_), channel_id=1, source_target_pairs={{0,1},{1,0},{2,3},{3,2},{4,5},{5,4},{6,7},{7,6},{8,9},{9,8},{10,11... | collective-permute-start | bytes 1376264 | tf_op jit(solution)/shard_map/ppermute | solution.py:302
  19.8 0.8 copy-start.3
  20.6 12.1 %collective-permute-start.10 = (bf16[448,512]{1,0:T(8,128)(2,1)}, bf16[448,512]{1,0:T(8,128)(2,1)S(1)}, u32[]{:S(2)}, u32[]{:S(2)}) collective-permute-start(bf16[448,512]{1,0:T(8,128)(2,1)} %collective-permute-done.8.refs_2_), channel_id=1, source_target_pairs={{0,2},{1,7},{2,4},{3,1},{4,6},{5,3},{6,0},{7,5},{8,10},{9,15},{10,... | collective-permute-start | bytes 1376264 | tf_op jit(solution)/shard_map/ppermute | solution.py:302
  20.6 21.7 %collective-permute-start.3 = (bf16[448,512]{1,0:T(8,128)(2,1)S(1)}, bf16[448,512]{1,0:T(8,128)(2,1)S(1)}, u32[]{:S(2)}, u32[]{:S(2)}) collective-permute-start(bf16[448,512]{1,0:T(8,128)(2,1)S(1)} %get-tuple-element.19.refs_2_), channel_id=1, source_target_pairs={{0,2},{1,7},{2,4},{3,1},{4,6},{5,3},{6,0},{7,5},{8,10},{9,15},{10,... | collective-permute-start | bytes 1376264 | tf_op jit(solution)/shard_map/ppermute | solution.py:302
  23.9 19.0 %collective-permute-start.5 = (bf16[448,512]{1,0:T(8,128)(2,1)S(1)}, bf16[448,512]{1,0:T(8,128)(2,1)}, u32[]{:S(2)}, u32[]{:S(2)}) collective-permute-start(bf16[448,512]{1,0:T(8,128)(2,1)S(1)} %collective-permute-done.refs_0_), channel_id=1, source_target_pairs={{0,6},{1,3},{2,0},{3,5},{4,2},{5,7},{6,4},{7,1},{8,14},{9,11},{10,... | collective-permute-start | bytes 1376264 | tf_op jit(solution)/shard_map/ppermute | solution.py:302
  23.9 19.2 %collective-permute-start.1 = (bf16[448,512]{1,0:T(8,128)(2,1)S(1)}, bf16[448,512]{1,0:T(8,128)(2,1)}, u32[]{:S(2)}, u32[]{:S(2)}) collective-permute-start(bf16[448,512]{1,0:T(8,128)(2,1)S(1)} %collective-permute-done.refs_0_), channel_id=1, source_target_pairs={{0,1},{1,0},{2,3},{3,2},{4,5},{5,4},{6,7},{7,6},{8,9},{9,8},{10,11... | collective-permute-start | bytes 1376264 | tf_op jit(solution)/shard_map/ppermute | solution.py:302
  24.9 21.3 %collective-permute-start.13 = (bf16[448,512]{1,0:T(8,128)(2,1)S(1)}, bf16[448,512]{1,0:T(8,128)(2,1)S(1)}, u32[]{:S(2)}, u32[]{:S(2)}) collective-permute-start(bf16[448,512]{1,0:T(8,128)(2,1)S(1)} %collective-permute-done.12.refs_2_), channel_id=1, source_target_pairs={{0,1},{1,0},{2,3},{3,2},{4,5},{5,4},{6,7},{7,6},{8,9},{9,8},{10,11... | collective-permute-start | bytes 1376264 | tf_op jit(solution)/shard_map/ppermute | solution.py:302
  32.7 13.5 %collective-permute-start.11 = (bf16[448,512]{1,0:T(8,128)(2,1)S(1)}, bf16[448,512]{1,0:T(8,128)(2,1)S(1)}, u32[]{:S(2)}, u32[]{:S(2)}) collective-permute-start(bf16[448,512]{1,0:T(8,128)(2,1)S(1)} %collective-permute-done.10.refs_0_), channel_id=1, source_target_pairs={{0,1},{1,0},{2,3},{3,2},{4,5},{5,4},{6,7},{7,6},{8,9},{9,8},{10,11... | collective-permute-start | bytes 1376264 | tf_op jit(solution)/shard_map/ppermute | solution.py:302
  32.9 3.1 %copy-start = (bf16[3584,1000]{0,1:T(8,128)(2,1)S(1)}, bf16[3584,1000]{0,1:T(8,128)(2,1)}, u32[]{:S(2)}) copy-start(bf16[3584,1000]{0,1:T(8,128)(2,1)} %param.9) | copy-start | bytes 21504004
  36.0 0.7 copy-start.5
  36.7 2.4 %copy-start.4 = (bf16[448,512]{1,0:T(8,128)(2,1)S(1)}, bf16[448,512]{1,0:T(8,128)(2,1)}, u32[]{:S(2)}) copy-start(bf16[448,512]{1,0:T(8,128)(2,1)} %copy-done.3) | copy-start | bytes 1376260
  42.3 3.9 %copy-start.1 = (s32[1024,128]{1,0:T(8,128)S(1)}, s32[1024,128]{1,0:T(8,128)}, u32[]{:S(2)}) copy-start(s32[1024,128]{1,0:T(8,128)} %ids_ref.3) | copy-start | bytes 1572868
  42.4 3.9 %copy-start.2 = (f32[1024,128]{1,0:T(8,128)S(1)}, f32[1024,128]{1,0:T(8,128)}, u32[]{:S(2)}) copy-start(f32[1024,128]{1,0:T(8,128)} %probs_ref.3) | copy-start | bytes 1572868
  42.4 7.9 %collective-permute-start.4 = (bf16[448,512]{1,0:T(8,128)(2,1)S(1)}, bf16[448,512]{1,0:T(8,128)(2,1)S(1)}, u32[]{:S(2)}, u32[]{:S(2)}) collective-permute-start(bf16[448,512]{1,0:T(8,128)(2,1)S(1)} %collective-permute-done.3.refs_0_), channel_id=1, source_target_pairs={{0,1},{1,0},{2,3},{3,2},{4,5},{5,4},{6,7},{7,6},{8,9},{9,8},{10,11... | collective-permute-start | bytes 1376264 | tf_op jit(solution)/shard_map/ppermute | solution.py:302
  42.8 7.4 %collective-permute-start.6 = (bf16[448,512]{1,0:T(8,128)(2,1)}, bf16[448,512]{1,0:T(8,128)(2,1)S(1)}, u32[]{:S(2)}, u32[]{:S(2)}) collective-permute-start(bf16[448,512]{1,0:T(8,128)(2,1)} %collective-permute-done.5.refs_2_), channel_id=1, source_target_pairs={{0,1},{1,0},{2,3},{3,2},{4,5},{5,4},{6,7},{7,6},{8,9},{9,8},{10,11... | collective-permute-start | bytes 1376264 | tf_op jit(solution)/shard_map/ppermute | solution.py:302
  50.2 11.9 %copy-start.6 = (s32[1024]{0:T(1024)S(1)}, s32[1024]{0:T(1024)}, u32[]{:S(2)}) copy-start(s32[1024]{0:T(1024)} %param.12) | copy-start | bytes 12292
  50.2 11.9 %copy-start.7 = (s32[8,2]{0,1:T(2,128)S(1)}, s32[8,2]{0,1:T(2,128)}, u32[]{:S(2)}) copy-start(s32[8,2]{0,1:T(2,128)} %param.13) | copy-start | bytes 196

commit v2 on v1

--- a/solution.py
+++ b/solution.py
@@ -70,23 +70,18 @@
 def squares_of(pieces):
     total = 0.0
     for piece in pieces:
-        for i in range(0, piece[0].shape[0], 16):
-            wide = across(piece, i, 16).astype(jnp.float32)
+        for i in range(0, piece.shape[0], 16):
+            wide = piece[i : i + 16, :].astype(jnp.float32)
             total = total + wide * wide
     return total
 
 
-def across(piece, start, count):
-    parts = [part[start : start + count, :] for part in piece]
-    return parts[0] if len(parts) == 1 else jnp.concatenate(parts, axis=1)
-
-
 def multiply(core, weight_ref, first, pieces):
-    shard = pieces[0][0].shape[0]
+    shard = pieces[0].shape[0]
     start, depth = first * CORES * shard, len(pieces) * shard
     rows = []
     for own, other in zip(pieces[::CORES], pieces[1::CORES]):
-        own, other = across(own, 0, shard), across(other, 0, shard)
+        own, other = own[...], other[...]
         rows += [jnp.where(core == 0, own, other), jnp.where(core == 0, other, own)]
     return jnp.dot(
         weight_ref[:, start : start + depth],
@@ -95,8 +90,51 @@
     )
 
 
+def multiply_side(core, weight_ref, first, pieces):
+    shard, width = pieces[0].shape
+    wide = -(-shard // LANES) * LANES
+    rest = jnp.zeros((wide - shard, width), jnp.bfloat16)
+    rows, columns = [], []
+    for k, piece in enumerate(pieces):
+        start = (first + k) * CORES * shard + core * (CORES * shard - wide)
+        columns.append(weight_ref[:, pl.ds(pl.multiple_of(start, LANES), wide)])
+        low = jnp.concatenate([piece[...], rest], axis=0)
+        high = jnp.concatenate([rest, piece[...]], axis=0)
+        rows.append(jnp.where(core == 0, low, high))
+    return jnp.dot(
+        jnp.concatenate(columns, axis=1),
+        jnp.concatenate(rows, axis=0),
+        preferred_element_type=jnp.float32,
+    )
+
+
+def middle_kernel(first, where_ref, weight_ref, near_ref, near_squares_ref, *refs):
+    pieces, (logits_ref, squares_ref) = refs[:-2], refs[-2:]
+    squares_ref[...] = near_squares_ref[...] + squares_of(pieces)
+    logits_ref[...] = near_ref[...] + multiply_side(where_ref[1], weight_ref, first, pieces)
+
+
+def middle(first, where, weight, near, squares, pieces):
+    vmem = pl.BlockSpec(memory_space=pltpu.VMEM)
+    vocab, width = near.shape
+    depth = len(pieces) * pieces[0].shape[0]
+    return pl.pallas_call(
+        functools.partial(middle_kernel, first),
+        out_shape=tuple(jax.ShapeDtypeStruct(a.shape, a.dtype) for a in (near, squares)),
+        in_specs=[pl.BlockSpec(memory_space=pltpu.SMEM)] + [vmem] * (3 + len(pieces)),
+        out_specs=(vmem, vmem),
+        compiler_params=pltpu.CompilerParams(vmem_limit_bytes=24 * MIB),
+        cost_estimate=pl.CostEstimate(
+            flops=2 * vocab * depth * width,
+            bytes_accessed=2 * (vocab + width) * depth + 8 * vocab * width,
+            transcendentals=0,
+        ),
+        name="middle",
+    )(where, weight, near, squares, *pieces)
+
+
 def near_kernel(first, where_ref, weight_ref, *refs):
-    pieces, (logits_ref, squares_ref) = [(p,) for p in refs[:-2]], refs[-2:]
+    pieces, (logits_ref, squares_ref) = refs[:-2], refs[-2:]
     squares_ref[...] = squares_of(pieces)
     logits_ref[...] = multiply(where_ref[1], weight_ref, first, pieces)
 
@@ -124,11 +162,8 @@
     )(where, weight, *pieces)
 
 
-def far_kernel(chunk, first, features, counts, where_ref, weight_ref, near_ref, squares_ref, ids_ref, probs_ref, *refs):
-    pieces = []
-    for count in counts:
-        pieces.append(refs[:count])
-        refs = refs[count:]
+def far_kernel(chunk, first, features, count, where_ref, weight_ref, near_ref, squares_ref, ids_ref, probs_ref, *refs):
+    pieces, refs = refs[:count], refs[count:]
     earlier = refs[0] if chunk else None
     outs, (logits_ref, scale_ref) = refs[bool(chunk) : -2], refs[-2:]
     vocab, width = near_ref.shape
@@ -136,7 +171,11 @@
     mean = jnp.sum(squares, axis=0, keepdims=True) * (1.0 / features)
     scale = lax.rsqrt(mean + EPS) * (1.0 / SOFTCAP)
     scale_ref[...] = jnp.broadcast_to(scale, scale_ref.shape)
-    logits_ref[...] = near_ref[...] + multiply(where_ref[1], weight_ref, first, pieces)
+    if chunk == 0:
+        late = multiply(where_ref[1], weight_ref, first, pieces)
+    else:
+        late = multiply_side(1 - where_ref[1], weight_ref, first, pieces)
+    logits_ref[...] = near_ref[...] + late
 
     blocks = width // BLOCK
     expsums, picks = [], []
@@ -188,8 +227,7 @@
 
 def far_head(chunk, first, where, weight, near, squares, ids, probs, pieces, earlier, peers):
     vocab, width = near.shape
-    counts = [len(piece) for piece in pieces]
-    shard = pieces[0][0].shape[0]
+    shard = pieces[0].shape[0]
     features = shard * CORES * CHIPS
     blocks = ids.shape[0] // BLOCK
     stat = lambda *shape: jax.ShapeDtypeStruct(shape, jnp.float32)
@@ -198,11 +236,10 @@
     else:
         out_shape = (stat(peers, 2 * blocks, BLOCK),)
     vmem = pl.BlockSpec(memory_space=pltpu.VMEM)
-    parts = [part for piece in pieces for part in piece]
-    operands = [weight, near, squares, ids, probs, *parts] + ([earlier] if chunk else [])
+    operands = [weight, near, squares, ids, probs, *pieces] + ([earlier] if chunk else [])
     depth = len(pieces) * shard
     return pl.pallas_call(
-        functools.partial(far_kernel, chunk, first, features, counts),
+        functools.partial(far_kernel, chunk, first, features, len(pieces)),
         out_shape=out_shape,
         in_specs=[pl.BlockSpec(memory_space=pltpu.SMEM)] + [vmem] * len(operands),
         out_specs=(vmem,) * len(out_shape),
@@ -323,10 +360,9 @@
     near1 = near_head(0, where, weight, (b1, b1s, second, z1))
     near0 = near_head(1, where, weight, (first, z0, a0, a0s))
     teacher = (teacher_ids, teacher_probs)
-    earlier, mass = far_head(
-        0, 3, where, weight, *near0, *teacher, ((c0,), (c0s,), (b0,), (b0s,)), None, peers
-    )
-    late = ((a1,), (a1s,), (c1,), (c1s,))
+    earlier, mass = far_head(0, 3, where, weight, *near0, *teacher, (c0, c0s, b0, b0s), None, peers)
+    near1 = middle(2, where, weight, *near1, (a1, c1))
+    late = (a1s, c1s)
     (copies,) = far_head(
         1, 2, where, weight, *near1, *teacher, late, earlier, peers
     )

time: 80.8 us -> 81.9 us (1.014)
  Pallas kernels: 18.5 us -> 19.6 us
    pallas_call x2 -> x3, Pallas kernels: 8.41 us -> 9.45 us  [the longest x2 7.08 us: far_head(): pl.pallas_call(functools.partial(far_kernel, chunk, first, features, len(...]
  transfers between devices with their start and end apart: 14 -> 14, of which waited for: 3 -> 3; matrix products, arithmetic and copies ran while one was open for 0% -> 0% of each run, Pallas kernels for 16% -> 18%
where the time goes in v2:
time: 81.9 us; the launch traced here: 81.6 us
  blocking collectives  24.3 us (30%)
  Pallas kernels  19.6 us (24%)
  starting transfers between devices  15.6 us (19%)
  waiting for transfers between devices  15.3 us (19%)
  local copies, waits for them, and re-layouts  5.86 us (7%)
    all_to_all x1, blocking collectives, per_device(): lax.all_to_all(message, 'seq', split_axis=0, concat_axis=0, tiled=True)  16.9 us
    ppermute x14, starting transfers between devices, move(): return lax.ppermute(x, 'vocab', pairs)  15.6 us
    ppermute x14, waiting for transfers between devices, move(): return lax.ppermute(x, 'vocab', pairs)  15.3 us
    all_to_all x1, blocking collectives, per_device(): lax.all_to_all(copies, 'vocab', split_axis=0, concat_axis=0, tiled=True)  7.44 us
    pallas_call x2, Pallas kernels, far_head(): pl.pallas_call(functools.partial(far_kernel, chunk, first, features, len(...  7.08 us
    pallas_call x2, Pallas kernels, near_head(): pl.pallas_call(functools.partial(near_kernel, first), out_shape=(jax.Shap...  6.31 us
    unnamed x17, local copies, waits for them, and re-layouts  4.57 us
    pallas_call x1, Pallas kernels, prepare(): pl.pallas_call(prepare_kernel, out_shape=jax.ShapeDtypeStruct((vocab, fea...  2.43 us
  transfers between devices with their start and end apart: 14, of which 3 were waited for; matrix products, arithmetic and copies ran while one was open for 0% of the time, Pallas kernels for 18%

profile of v2, /device:TPU:1, one launch (start us, length us, event | category | flops | bytes accessed | tf_op | source)
XLA Modules:
  0.0 81.6 jit_solution(11678700404680369350)
XLA Ops:
  0.6 1.2 %fusion = (bf16[448,512]{1,0:T(8,128)(2,1)S(1)}, bf16[448,512]{1,0:T(8,128)(2,1)S(1)}) fusion(bf16[448,1024]{1,0:T(8,128)(2,1)} %bitcast.20), kind=kLoop, calls=%fused_computation.2 | loop fusion | bytes 1835008 | tf_op jit(solution)/shard_map/slice | solution.py:349
  1.9 3.6 %collective-permute-start.8 = (bf16[448,512]{1,0:T(8,128)(2,1)S(1)}, bf16[448,512]{1,0:T(8,128)(2,1)}, u32[]{:S(2)}, u32[]{:S(2)}) collective-permute-start(bf16[448,512]{1,0:T(8,128)(2,1)S(1)} %get-tuple-element.22.refs_0_), channel_id=1, source_target_pairs={{0,2},{1,7},{2,4},{3,1},{4,6},{5,3},{6,0},{7,5},{8,10},{9,15},{10,... | collective-permute-start | bytes 1376264 | tf_op jit(solution)/shard_map/ppermute | solution.py:339
  5.5 0.0 collective-permute-start.7
  5.5 0.8 collective-permute-start.12
  6.3 1.0 %collective-permute-start = (bf16[448,512]{1,0:T(8,128)(2,1)S(1)}, bf16[448,512]{1,0:T(8,128)(2,1)S(1)}, u32[]{:S(2)}, u32[]{:S(2)}) collective-permute-start(bf16[448,512]{1,0:T(8,128)(2,1)S(1)} %get-tuple-element.23.refs_2_), channel_id=1, source_target_pairs={{0,6},{1,3},{2,0},{3,5},{4,2},{5,7},{6,4},{7,1},{8,14},{9,11},{10,... | collective-permute-start | bytes 1376264 | tf_op jit(solution)/shard_map/ppermute | solution.py:339
  7.3 1.2 %collective-permute-start.2 = (bf16[448,512]{1,0:T(8,128)(2,1)S(1)}, bf16[448,512]{1,0:T(8,128)(2,1)S(1)}, u32[]{:S(2)}, u32[]{:S(2)}) collective-permute-start(bf16[448,512]{1,0:T(8,128)(2,1)S(1)} %get-tuple-element.23.refs_2_), channel_id=1, source_target_pairs={{0,1},{1,0},{2,3},{3,2},{4,5},{5,4},{6,7},{7,6},{8,9},{9,8},{10,11... | collective-permute-start | bytes 1376264 | tf_op jit(solution)/shard_map/ppermute | solution.py:339
  8.5 4.3 %collective-permute-done.8.refs_2_ = bf16[448,512]{1,0:T(8,128)(2,1)} collective-permute-done((bf16[448,512]{1,0:T(8,128)(2,1)S(1)}, bf16[448,512]{1,0:T(8,128)(2,1)}, u32[]{:S(2)}, u32[]{:S(2)}) %collective-permute-start.8) | collective-permute-done | bytes 458784 | tf_op jit(solution)/shard_map/ppermute | solution.py:339
  12.7 7.1 %collective-permute-start.9 = (bf16[448,512]{1,0:T(8,128)(2,1)}, bf16[448,512]{1,0:T(8,128)(2,1)}, u32[]{:S(2)}, u32[]{:S(2)}) collective-permute-start(bf16[448,512]{1,0:T(8,128)(2,1)} %collective-permute-done.8.refs_2_), channel_id=1, source_target_pairs={{0,1},{1,0},{2,3},{3,2},{4,5},{5,4},{6,7},{7,6},{8,9},{9,8},{10,11... | collective-permute-start | bytes 1376264 | tf_op jit(solution)/shard_map/ppermute | solution.py:339
  19.8 0.0 collective-permute-done.7.refs_1_
  19.8 0.0 copy-start.3
  19.8 0.8 copy-done.3
  20.6 0.0 collective-permute-start.10
  20.6 0.0 collective-permute-done.12.refs_2_
  20.6 0.0 collective-permute-start.3
  20.6 3.2 %collective-permute-done.refs_0_ = bf16[448,512]{1,0:T(8,128)(2,1)S(1)} collective-permute-done((bf16[448,512]{1,0:T(8,128)(2,1)S(1)}, bf16[448,512]{1,0:T(8,128)(2,1)S(1)}, u32[]{:S(2)}, u32[]{:S(2)}) %collective-permute-start) | collective-permute-done | bytes 458784 | tf_op jit(solution)/shard_map/ppermute | solution.py:339
  23.9 0.0 collective-permute-start.4
  23.9 0.0 collective-permute-done.2.refs_3_
  23.9 1.0 %collective-permute-start.1 = (bf16[448,512]{1,0:T(8,128)(2,1)S(1)}, bf16[448,512]{1,0:T(8,128)(2,1)}, u32[]{:S(2)}, u32[]{:S(2)}) collective-permute-start(bf16[448,512]{1,0:T(8,128)(2,1)S(1)} %collective-permute-done.refs_0_), channel_id=1, source_target_pairs={{0,1},{1,0},{2,3},{3,2},{4,5},{5,4},{6,7},{7,6},{8,9},{9,8},{10,11... | collective-permute-start | bytes 1376264 | tf_op jit(solution)/shard_map/ppermute | solution.py:339
  24.8 0.1 pad_add_fusion.where_ref
  24.9 0.0 collective-permute-done.9.refs_3_
  24.9 0.0 collective-permute-start.13
  24.9 7.8 %collective-permute-done.10.refs_0_ = bf16[448,512]{1,0:T(8,128)(2,1)S(1)} collective-permute-done((bf16[448,512]{1,0:T(8,128)(2,1)}, bf16[448,512]{1,0:T(8,128)(2,1)S(1)}, u32[]{:S(2)}, u32[]{:S(2)}) %collective-permute-start.10) | collective-permute-done | bytes 458784 | tf_op jit(solution)/shard_map/ppermute | solution.py:339
  32.7 0.2 collective-permute-start.11
  32.9 0.0 copy-start
  32.9 3.0 %copy-done = bf16[3584,1000]{0,1:T(8,128)(2,1)S(1)} copy-done((bf16[3584,1000]{0,1:T(8,128)(2,1)S(1)}, bf16[3584,1000]{0,1:T(8,128)(2,1)}, u32[]{:S(2)}) %copy-start) | copy-done | bytes 7168024
  35.9 0.0 copy-start.5
  35.9 0.7 copy-done.5
  36.6 0.0 copy-start.4
  36.6 2.4 %prepare.1.weight_ref = bf16[1000,4480]{1,0:T(8,128)(2,1)S(1)} custom-call(s32[3]{0:T(128)S(1)} %pad_add_fusion.where_ref, bf16[1000,3584]{1,0:T(8,128)(2,1)S(1)} %bitcast.14, f32[28,128]{1,0:T(8,128)S(1)} %bitcast.17), custom_call_target="tpu_custom_call" | custom-call | flops 1792000000 | bytes 14336000 | tf_op jit(solution)/shard_map/prepare/pallas_call | solution.py:57
  39.1 0.0 copy-done.4
  39.1 3.2 %near.3 = (f32[1000,512]{1,0:T(8,128)S(1)}, f32[16,512]{1,0:T(8,128)S(1)}) custom-call(s32[3]{0:T(128)S(1)} %pad_add_fusion.where_ref, bf16[1000,4480]{1,0:T(8,128)(2,1)S(1)} %prepare.1.weight_ref, bf16[448,512]{1,0:T(8,128)(2,1)S(1)} %get-tuple-element.22.refs_0_, bf16[448,512]{1,0:T(8,128)(2,1)S(1)} %copy-done.4, ...), custom_call_target="tpu_custom_call" | custom-call | flops 1835008000 | bytes 5419008 | tf_op jit(solution)/shard_map/near/pallas_call | solution.py:147
  42.3 0.0 collective-permute-done.3.refs_0_
  42.3 0.4 collective-permute-start.5
  42.8 0.0 collective-permute-done.4.refs_1_
  42.8 0.3 collective-permute-start.6
  43.1 0.0 collective-permute-done.1.refs_1_
  43.1 3.1 %near.2 = (f32[1000,512]{1,0:T(8,128)S(1)}, f32[16,512]{1,0:T(8,128)S(1)}) custom-call(s32[3]{0:T(128)S(1)} %pad_add_fusion.where_ref, bf16[1000,4480]{1,0:T(8,128)(2,1)S(1)} %prepare.1.weight_ref, bf16[448,512]{1,0:T(8,128)(2,1)S(1)} %collective-permute-done.refs_0_, bf16[448,512]{1,0:T(8,128)(2,1)} %collective-permute-done.1.refs_1_, ...), custom_call_target="tpu_custom_call" | custom-call | flops 1835008000 | bytes 5419008 | tf_op jit(solution)/shard_map/near/pallas_call | solution.py:147
  46.1 0.0 copy-start.1
  46.2 0.0 copy-start.2
  46.2 2.4 %middle.1 = (f32[1000,512]{1,0:T(8,128)S(1)}, f32[16,512]{1,0:T(8,128)S(1)}) custom-call(s32[3]{0:T(128)S(1)} %pad_add_fusion.where_ref, bf16[1000,4480]{1,0:T(8,128)(2,1)S(1)} %prepare.1.weight_ref, f32[1000,512]{1,0:T(8,128)S(1)} %get-tuple-element.12.near_ref, f32[16,512]{1,0:T(8,128)S(1)} %get-tuple-element.13.near_squares_ref, ...), custom_call_target="tpu_custom_call" | custom-call | flops 917504000 | bytes 6805504 | tf_op jit(solution)/shard_map/middle/pallas_call | solution.py:121
  48.5 0.0 collective-permute-done.13.refs_3_
  48.6 0.0 collective-permute-done.11.refs_1_
  48.6 0.0 copy-done.1
  48.6 0.0 copy-done.2
  48.6 4.0 %far.2 = (f32[8,128]{1,0:T(8,128)S(1)}, f32[8,128]{1,0:T(8,128)S(1)}) custom-call(s32[3]{0:T(128)S(1)} %pad_add_fusion.where_ref, bf16[1000,4480]{1,0:T(8,128)(2,1)S(1)} %prepare.1.weight_ref, f32[1000,512]{1,0:T(8,128)S(1)} %get-tuple-element.16.near_ref, f32[16,512]{1,0:T(8,128)S(1)} %get-tuple-element.17.squares_ref, s32[1024,128]{1,0:T(8,128)S(1)} %copy-done.1, ...), custom_call_target="tpu_custom_call" | custom-call | flops 3670016000 | bytes 9515008 | tf_op jit(solution)/shard_map/far/pallas_call | solution.py:241
  52.6 0.0 collective-permute-done.5.refs_0_
  52.6 0.0 collective-permute-done.6.refs_1_
  52.6 0.0 copy-start.6
  52.6 0.0 copy-start.7
  52.6 3.1 %far.3 = f32[8,16,128]{2,1,0:T(8,128)S(1)} custom-call(s32[3]{0:T(128)S(1)} %pad_add_fusion.where_ref, bf16[1000,4480]{1,0:T(8,128)(2,1)S(1)} %prepare.1.weight_ref, f32[1000,512]{1,0:T(8,128)S(1)} %get-tuple-element.14.near_ref, f32[16,512]{1,0:T(8,128)S(1)} %get-tuple-element.15.squares_ref, s32[1024,128]{1,0:T(8,128)S(1)} %copy-done.1, ...), custom_call_target="tpu_custom_call" | custom-call | flops 1835008000 | bytes 6805504 | tf_op jit(solution)/shard_map/far/pallas_call | solution.py:241
  55.7 7.4 %all_to_all.16.came_ref = f32[8,16,128]{2,1,0:T(8,128)S(1)} all-to-all(f32[8,16,128]{2,1,0:T(8,128)S(1)} %far.3), channel_id=1, replica_groups=mesh['seq'=32,'vocab'=8] {'vocab'}, dimensions={0} | all-to-all | bytes 131072 | tf_op jit(solution)/shard_map/all_to_all | solution.py:370
  63.2 0.0 copy-done.6
  63.2 0.0 copy-done.7
  63.2 0.8 losses.1
  64.0 0.1 copy.9
  64.0 16.9 %all_to_all.17 = f32[32,1,512]{2,1,0:T(1,128)S(1)} all-to-all(f32[32,1,512]{2,1,0:T(1,128)S(1)} %copy.9), channel_id=1, replica_groups=mesh['seq'=32,'vocab'=8] {'seq'}, dimensions={0} | all-to-all | bytes 131072 | tf_op jit(solution)/shard_map/all_to_all | solution.py:372
  81.0 0.6 finish.1
  (1 shorter events, 0.0 us)
Async XLA Ops:
  1.9 10.9 %collective-permute-start.8 = (bf16[448,512]{1,0:T(8,128)(2,1)S(1)}, bf16[448,512]{1,0:T(8,128)(2,1)}, u32[]{:S(2)}, u32[]{:S(2)}) collective-permute-start(bf16[448,512]{1,0:T(8,128)(2,1)S(1)} %get-tuple-element.22.refs_0_), channel_id=1, source_target_pairs={{0,2},{1,7},{2,4},{3,1},{4,6},{5,3},{6,0},{7,5},{8,10},{9,15},{10,... | collective-permute-start | bytes 1376264 | tf_op jit(solution)/shard_map/ppermute | solution.py:339
  5.5 14.4 %collective-permute-start.7 = (bf16[448,512]{1,0:T(8,128)(2,1)S(1)}, bf16[448,512]{1,0:T(8,128)(2,1)S(1)}, u32[]{:S(2)}, u32[]{:S(2)}) collective-permute-start(bf16[448,512]{1,0:T(8,128)(2,1)S(1)} %get-tuple-element.22.refs_0_), channel_id=1, source_target_pairs={{0,1},{1,0},{2,3},{3,2},{4,5},{5,4},{6,7},{7,6},{8,9},{9,8},{10,11... | collective-permute-start | bytes 1376264 | tf_op jit(solution)/shard_map/ppermute | solution.py:339
  5.5 15.1 %collective-permute-start.12 = (bf16[448,512]{1,0:T(8,128)(2,1)S(1)}, bf16[448,512]{1,0:T(8,128)(2,1)S(1)}, u32[]{:S(2)}, u32[]{:S(2)}) collective-permute-start(bf16[448,512]{1,0:T(8,128)(2,1)S(1)} %get-tuple-element.22.refs_0_), channel_id=1, source_target_pairs={{0,6},{1,3},{2,0},{3,5},{4,2},{5,7},{6,4},{7,1},{8,14},{9,11},{10,... | collective-permute-start | bytes 1376264 | tf_op jit(solution)/shard_map/ppermute | solution.py:339
  6.3 17.6 %collective-permute-start = (bf16[448,512]{1,0:T(8,128)(2,1)S(1)}, bf16[448,512]{1,0:T(8,128)(2,1)S(1)}, u32[]{:S(2)}, u32[]{:S(2)}) collective-permute-start(bf16[448,512]{1,0:T(8,128)(2,1)S(1)} %get-tuple-element.23.refs_2_), channel_id=1, source_target_pairs={{0,6},{1,3},{2,0},{3,5},{4,2},{5,7},{6,4},{7,1},{8,14},{9,11},{10,... | collective-permute-start | bytes 1376264 | tf_op jit(solution)/shard_map/ppermute | solution.py:339
  7.3 16.6 %collective-permute-start.2 = (bf16[448,512]{1,0:T(8,128)(2,1)S(1)}, bf16[448,512]{1,0:T(8,128)(2,1)S(1)}, u32[]{:S(2)}, u32[]{:S(2)}) collective-permute-start(bf16[448,512]{1,0:T(8,128)(2,1)S(1)} %get-tuple-element.23.refs_2_), channel_id=1, source_target_pairs={{0,1},{1,0},{2,3},{3,2},{4,5},{5,4},{6,7},{7,6},{8,9},{9,8},{10,11... | collective-permute-start | bytes 1376264 | tf_op jit(solution)/shard_map/ppermute | solution.py:339
  12.7 12.2 %collective-permute-start.9 = (bf16[448,512]{1,0:T(8,128)(2,1)}, bf16[448,512]{1,0:T(8,128)(2,1)}, u32[]{:S(2)}, u32[]{:S(2)}) collective-permute-start(bf16[448,512]{1,0:T(8,128)(2,1)} %collective-permute-done.8.refs_2_), channel_id=1, source_target_pairs={{0,1},{1,0},{2,3},{3,2},{4,5},{5,4},{6,7},{7,6},{8,9},{9,8},{10,11... | collective-permute-start | bytes 1376264 | tf_op jit(solution)/shard_map/ppermute | solution.py:339
  19.8 0.8 copy-start.3
  20.6 12.1 %collective-permute-start.10 = (bf16[448,512]{1,0:T(8,128)(2,1)}, bf16[448,512]{1,0:T(8,128)(2,1)S(1)}, u32[]{:S(2)}, u32[]{:S(2)}) collective-permute-start(bf16[448,512]{1,0:T(8,128)(2,1)} %collective-permute-done.8.refs_2_), channel_id=1, source_target_pairs={{0,2},{1,7},{2,4},{3,1},{4,6},{5,3},{6,0},{7,5},{8,10},{9,15},{10,... | collective-permute-start | bytes 1376264 | tf_op jit(solution)/shard_map/ppermute | solution.py:339
  20.6 21.7 %collective-permute-start.3 = (bf16[448,512]{1,0:T(8,128)(2,1)S(1)}, bf16[448,512]{1,0:T(8,128)(2,1)S(1)}, u32[]{:S(2)}, u32[]{:S(2)}) collective-permute-start(bf16[448,512]{1,0:T(8,128)(2,1)S(1)} %get-tuple-element.23.refs_2_), channel_id=1, source_target_pairs={{0,2},{1,7},{2,4},{3,1},{4,6},{5,3},{6,0},{7,5},{8,10},{9,15},{10,... | collective-permute-start | bytes 1376264 | tf_op jit(solution)/shard_map/ppermute | solution.py:339
  23.9 18.9 %collective-permute-start.4 = (bf16[448,512]{1,0:T(8,128)(2,1)S(1)}, bf16[448,512]{1,0:T(8,128)(2,1)}, u32[]{:S(2)}, u32[]{:S(2)}) collective-permute-start(bf16[448,512]{1,0:T(8,128)(2,1)S(1)} %collective-permute-done.refs_0_), channel_id=1, source_target_pairs={{0,6},{1,3},{2,0},{3,5},{4,2},{5,7},{6,4},{7,1},{8,14},{9,11},{10,... | collective-permute-start | bytes 1376264 | tf_op jit(solution)/shard_map/ppermute | solution.py:339
  23.9 19.2 %collective-permute-start.1 = (bf16[448,512]{1,0:T(8,128)(2,1)S(1)}, bf16[448,512]{1,0:T(8,128)(2,1)}, u32[]{:S(2)}, u32[]{:S(2)}) collective-permute-start(bf16[448,512]{1,0:T(8,128)(2,1)S(1)} %collective-permute-done.refs_0_), channel_id=1, source_target_pairs={{0,1},{1,0},{2,3},{3,2},{4,5},{5,4},{6,7},{7,6},{8,9},{9,8},{10,11... | collective-permute-start | bytes 1376264 | tf_op jit(solution)/shard_map/ppermute | solution.py:339
  24.9 23.6 %collective-permute-start.13 = (bf16[448,512]{1,0:T(8,128)(2,1)S(1)}, bf16[448,512]{1,0:T(8,128)(2,1)S(1)}, u32[]{:S(2)}, u32[]{:S(2)}) collective-permute-start(bf16[448,512]{1,0:T(8,128)(2,1)S(1)} %collective-permute-done.12.refs_2_), channel_id=1, source_target_pairs={{0,1},{1,0},{2,3},{3,2},{4,5},{5,4},{6,7},{7,6},{8,9},{9,8},{10,11... | collective-permute-start | bytes 1376264 | tf_op jit(solution)/shard_map/ppermute | solution.py:339
  32.7 15.9 %collective-permute-start.11 = (bf16[448,512]{1,0:T(8,128)(2,1)S(1)}, bf16[448,512]{1,0:T(8,128)(2,1)S(1)}, u32[]{:S(2)}, u32[]{:S(2)}) collective-permute-start(bf16[448,512]{1,0:T(8,128)(2,1)S(1)} %collective-permute-done.10.refs_0_), channel_id=1, source_target_pairs={{0,1},{1,0},{2,3},{3,2},{4,5},{5,4},{6,7},{7,6},{8,9},{9,8},{10,11... | collective-permute-start | bytes 1376264 | tf_op jit(solution)/shard_map/ppermute | solution.py:339
  32.9 3.1 %copy-start = (bf16[3584,1000]{0,1:T(8,128)(2,1)S(1)}, bf16[3584,1000]{0,1:T(8,128)(2,1)}, u32[]{:S(2)}) copy-start(bf16[3584,1000]{0,1:T(8,128)(2,1)} %param.9) | copy-start | bytes 21504004
  35.9 0.7 copy-start.5
  36.6 2.4 %copy-start.4 = (bf16[448,512]{1,0:T(8,128)(2,1)S(1)}, bf16[448,512]{1,0:T(8,128)(2,1)}, u32[]{:S(2)}) copy-start(bf16[448,512]{1,0:T(8,128)(2,1)} %copy-done.3) | copy-start | bytes 1376260
  42.3 10.2 %collective-permute-start.5 = (bf16[448,512]{1,0:T(8,128)(2,1)S(1)}, bf16[448,512]{1,0:T(8,128)(2,1)S(1)}, u32[]{:S(2)}, u32[]{:S(2)}) collective-permute-start(bf16[448,512]{1,0:T(8,128)(2,1)S(1)} %collective-permute-done.3.refs_0_), channel_id=1, source_target_pairs={{0,1},{1,0},{2,3},{3,2},{4,5},{5,4},{6,7},{7,6},{8,9},{9,8},{10,11... | collective-permute-start | bytes 1376264 | tf_op jit(solution)/shard_map/ppermute | solution.py:339
  42.8 9.8 %collective-permute-start.6 = (bf16[448,512]{1,0:T(8,128)(2,1)}, bf16[448,512]{1,0:T(8,128)(2,1)S(1)}, u32[]{:S(2)}, u32[]{:S(2)}) collective-permute-start(bf16[448,512]{1,0:T(8,128)(2,1)} %collective-permute-done.4.refs_1_), channel_id=1, source_target_pairs={{0,1},{1,0},{2,3},{3,2},{4,5},{5,4},{6,7},{7,6},{8,9},{9,8},{10,11... | collective-permute-start | bytes 1376264 | tf_op jit(solution)/shard_map/ppermute | solution.py:339
  46.1 2.4 %copy-start.1 = (s32[1024,128]{1,0:T(8,128)S(1)}, s32[1024,128]{1,0:T(8,128)}, u32[]{:S(2)}) copy-start(s32[1024,128]{1,0:T(8,128)} %ids_ref.3) | copy-start | bytes 1572868
  46.2 2.4 %copy-start.2 = (f32[1024,128]{1,0:T(8,128)S(1)}, f32[1024,128]{1,0:T(8,128)}, u32[]{:S(2)}) copy-start(f32[1024,128]{1,0:T(8,128)} %probs_ref.3) | copy-start | bytes 1572868
  52.6 10.6 %copy-start.6 = (s32[1024]{0:T(1024)S(1)}, s32[1024]{0:T(1024)}, u32[]{:S(2)}) copy-start(s32[1024]{0:T(1024)} %param.12) | copy-start | bytes 12292
  52.6 10.6 %copy-start.7 = (s32[8,2]{0,1:T(2,128)S(1)}, s32[8,2]{0,1:T(2,128)}, u32[]{:S(2)}) copy-start(s32[8,2]{0,1:T(2,128)} %param.13) | copy-start | bytes 196

commit v3 on v2

--- a/solution.py
+++ b/solution.py
@@ -18,6 +18,7 @@
 SOFTCAP = 30.0
 EPS = 1e-06
 LANES = 128
+BAND = 256
 MIB = 1 << 20
 
 
@@ -76,42 +77,57 @@
     return total
 
 
-def multiply(core, weight_ref, first, pieces):
-    shard = pieces[0].shape[0]
-    start, depth = first * CORES * shard, len(pieces) * shard
+def pair_rows(core, pieces):
     rows = []
     for own, other in zip(pieces[::CORES], pieces[1::CORES]):
         own, other = own[...], other[...]
         rows += [jnp.where(core == 0, own, other), jnp.where(core == 0, other, own)]
+    return jnp.concatenate(rows, axis=0)
+
+
+def pair_columns(weight_ref, first, pieces, band):
+    shard = pieces[0].shape[0]
+    start = first * CORES * shard
+    return weight_ref[band, start : start + len(pieces) * shard]
+
+
+def multiply(core, weight_ref, first, pieces):
     return jnp.dot(
-        weight_ref[:, start : start + depth],
-        jnp.concatenate(rows, axis=0),
+        pair_columns(weight_ref, first, pieces, slice(None)),
+        pair_rows(core, pieces),
         preferred_element_type=jnp.float32,
     )
 
 
-def multiply_side(core, weight_ref, first, pieces):
+def side_rows(core, pieces):
     shard, width = pieces[0].shape
-    wide = -(-shard // LANES) * LANES
-    rest = jnp.zeros((wide - shard, width), jnp.bfloat16)
-    rows, columns = [], []
-    for k, piece in enumerate(pieces):
-        start = (first + k) * CORES * shard + core * (CORES * shard - wide)
-        columns.append(weight_ref[:, pl.ds(pl.multiple_of(start, LANES), wide)])
+    rest = jnp.zeros((-shard % LANES, width), jnp.bfloat16)
+    rows = []
+    for piece in pieces:
         low = jnp.concatenate([piece[...], rest], axis=0)
         high = jnp.concatenate([rest, piece[...]], axis=0)
         rows.append(jnp.where(core == 0, low, high))
-    return jnp.dot(
-        jnp.concatenate(columns, axis=1),
-        jnp.concatenate(rows, axis=0),
-        preferred_element_type=jnp.float32,
-    )
+    return jnp.concatenate(rows, axis=0)
+
+
+def side_columns(core, weight_ref, first, pieces, band):
+    shard = pieces[0].shape[0]
+    wide = shard + -shard % LANES
+    columns = []
+    for k in range(len(pieces)):
+        start = (first + k) * CORES * shard + core * (CORES * shard - wide)
+        columns.append(weight_ref[band, pl.ds(pl.multiple_of(start, LANES), wide)])
+    return jnp.concatenate(columns, axis=1)
 
 
 def middle_kernel(first, where_ref, weight_ref, near_ref, near_squares_ref, *refs):
     pieces, (logits_ref, squares_ref) = refs[:-2], refs[-2:]
     squares_ref[...] = near_squares_ref[...] + squares_of(pieces)
-    logits_ref[...] = near_ref[...] + multiply_side(where_ref[1], weight_ref, first, pieces)
+    logits_ref[...] = near_ref[...] + jnp.dot(
+        side_columns(where_ref[1], weight_ref, first, pieces, slice(None)),
+        side_rows(where_ref[1], pieces),
+        preferred_element_type=jnp.float32,
+    )
 
 
 def middle(first, where, weight, near, squares, pieces):
@@ -165,23 +181,26 @@
 def far_kernel(chunk, first, features, count, where_ref, weight_ref, near_ref, squares_ref, ids_ref, probs_ref, *refs):
     pieces, refs = refs[:count], refs[count:]
     earlier = refs[0] if chunk else None
-    outs, (logits_ref, scale_ref) = refs[bool(chunk) : -2], refs[-2:]
+    outs, soft_ref = refs[bool(chunk) : -1], refs[-1]
     vocab, width = near_ref.shape
     squares = squares_ref[...] + squares_of(pieces)
     mean = jnp.sum(squares, axis=0, keepdims=True) * (1.0 / features)
     scale = lax.rsqrt(mean + EPS) * (1.0 / SOFTCAP)
-    scale_ref[...] = jnp.broadcast_to(scale, scale_ref.shape)
-    if chunk == 0:
-        late = multiply(where_ref[1], weight_ref, first, pieces)
-    else:
-        late = multiply_side(1 - where_ref[1], weight_ref, first, pieces)
-    logits_ref[...] = near_ref[...] + late
+    core = where_ref[1] if chunk == 0 else 1 - where_ref[1]
+    rows = pair_rows(core, pieces) if chunk == 0 else side_rows(core, pieces)
+    for start in range(0, vocab, BAND):
+        band = slice(start, min(start + BAND, vocab))
+        if chunk == 0:
+            columns = pair_columns(weight_ref, first, pieces, band)
+        else:
+            columns = side_columns(core, weight_ref, first, pieces, band)
+        late = jnp.dot(columns, rows, preferred_element_type=jnp.float32)
+        soft_ref[band, :] = jnp.tanh((near_ref[band, :] + late) * scale)
 
     blocks = width // BLOCK
     expsums, picks = [], []
     for q in range(blocks):
         lanes = slice(q * BLOCK, (q + 1) * BLOCK)
-        scale = scale_ref[0:1, lanes]
         rows = slice((chunk * blocks + q) * BLOCK, (chunk * blocks + q + 1) * BLOCK)
         within = ids_ref[rows, :] - where_ref[2]
         tile, spot = within >> 7, within & (LANES - 1)
@@ -189,7 +208,7 @@
         turned = []
         for t in range(-(-vocab // LANES)):
             size = min(LANES, vocab - t * LANES)
-            soft = jnp.tanh(logits_ref[t * LANES : t * LANES + size, lanes] * scale)
+            soft = soft_ref[t * LANES : t * LANES + size, lanes]
             power = jnp.exp(SOFTCAP * soft)
             sums = sums + jnp.sum(power.reshape(size // 8, 8, BLOCK), axis=0)
             if size < LANES:
@@ -243,10 +262,7 @@
         out_shape=out_shape,
         in_specs=[pl.BlockSpec(memory_space=pltpu.SMEM)] + [vmem] * len(operands),
         out_specs=(vmem,) * len(out_shape),
-        scratch_shapes=[
-            pltpu.VMEM((vocab, width), jnp.float32),
-            pltpu.VMEM((8, width), jnp.float32),
-        ],
+        scratch_shapes=[pltpu.VMEM((vocab, width), jnp.float32)],
         compiler_params=pltpu.CompilerParams(vmem_limit_bytes=24 * MIB),
         cost_estimate=pl.CostEstimate(
             flops=2 * 2 * vocab * depth * width,

time: 81.9 us -> 80.8 us (0.987)
  Pallas kernels: 19.6 us -> 18.5 us
    pallas_call x2, Pallas kernels: 7.08 us -> 5.97 us  [far_head(): pl.pallas_call(functools.partial(far_kernel, chunk, first, features, len(...]
where the time goes in v3:
time: 80.8 us; the launch traced here: 80.5 us
  blocking collectives  24.4 us (30%)
  Pallas kernels  18.5 us (23%)
  starting transfers between devices  15.6 us (19%)
  waiting for transfers between devices  15.3 us (19%)
  local copies, waits for them, and re-layouts  5.86 us (7%)
    all_to_all x1, blocking collectives, per_device(): lax.all_to_all(message, 'seq', split_axis=0, concat_axis=0, tiled=True)  16.9 us
    ppermute x14, starting transfers between devices, move(): return lax.ppermute(x, 'vocab', pairs)  15.6 us
    ppermute x14, waiting for transfers between devices, move(): return lax.ppermute(x, 'vocab', pairs)  15.3 us
    all_to_all x1, blocking collectives, per_device(): lax.all_to_all(copies, 'vocab', split_axis=0, concat_axis=0, tiled=True)  7.46 us
    pallas_call x2, Pallas kernels, near_head(): pl.pallas_call(functools.partial(near_kernel, first), out_shape=(jax.Shap...  6.31 us
    pallas_call x2, Pallas kernels, far_head(): pl.pallas_call(functools.partial(far_kernel, chunk, first, features, len(...  5.97 us
    unnamed x17, local copies, waits for them, and re-layouts  4.57 us
    pallas_call x1, Pallas kernels, prepare(): pl.pallas_call(prepare_kernel, out_shape=jax.ShapeDtypeStruct((vocab, fea...  2.43 us
  transfers between devices with their start and end apart: 14, of which 3 were waited for; matrix products, arithmetic and copies ran while one was open for 0% of the time, Pallas kernels for 18%

profile of v3, /device:TPU:1, one launch (start us, length us, event | category | flops | bytes accessed | tf_op | source)
XLA Modules:
  0.0 80.5 jit_solution(6314704380783168571)
XLA Ops:
  0.6 1.2 %fusion = (bf16[448,512]{1,0:T(8,128)(2,1)S(1)}, bf16[448,512]{1,0:T(8,128)(2,1)S(1)}) fusion(bf16[448,1024]{1,0:T(8,128)(2,1)} %bitcast.20), kind=kLoop, calls=%fused_computation.2 | loop fusion | bytes 1835008 | tf_op jit(solution)/shard_map/slice | solution.py:365
  1.9 3.6 %collective-permute-start.8 = (bf16[448,512]{1,0:T(8,128)(2,1)S(1)}, bf16[448,512]{1,0:T(8,128)(2,1)}, u32[]{:S(2)}, u32[]{:S(2)}) collective-permute-start(bf16[448,512]{1,0:T(8,128)(2,1)S(1)} %get-tuple-element.22.refs_0_), channel_id=1, source_target_pairs={{0,2},{1,7},{2,4},{3,1},{4,6},{5,3},{6,0},{7,5},{8,10},{9,15},{10,... | collective-permute-start | bytes 1376264 | tf_op jit(solution)/shard_map/ppermute | solution.py:355
  5.5 0.0 collective-permute-start.7
  5.5 0.8 %collective-permute-start.12 = (bf16[448,512]{1,0:T(8,128)(2,1)S(1)}, bf16[448,512]{1,0:T(8,128)(2,1)S(1)}, u32[]{:S(2)}, u32[]{:S(2)}) collective-permute-start(bf16[448,512]{1,0:T(8,128)(2,1)S(1)} %get-tuple-element.22.refs_0_), channel_id=1, source_target_pairs={{0,6},{1,3},{2,0},{3,5},{4,2},{5,7},{6,4},{7,1},{8,14},{9,11},{10,... | collective-permute-start | bytes 1376264 | tf_op jit(solution)/shard_map/ppermute | solution.py:355
  6.3 1.0 %collective-permute-start = (bf16[448,512]{1,0:T(8,128)(2,1)S(1)}, bf16[448,512]{1,0:T(8,128)(2,1)S(1)}, u32[]{:S(2)}, u32[]{:S(2)}) collective-permute-start(bf16[448,512]{1,0:T(8,128)(2,1)S(1)} %get-tuple-element.23.refs_2_), channel_id=1, source_target_pairs={{0,6},{1,3},{2,0},{3,5},{4,2},{5,7},{6,4},{7,1},{8,14},{9,11},{10,... | collective-permute-start | bytes 1376264 | tf_op jit(solution)/shard_map/ppermute | solution.py:355
  7.3 1.2 %collective-permute-start.2 = (bf16[448,512]{1,0:T(8,128)(2,1)S(1)}, bf16[448,512]{1,0:T(8,128)(2,1)S(1)}, u32[]{:S(2)}, u32[]{:S(2)}) collective-permute-start(bf16[448,512]{1,0:T(8,128)(2,1)S(1)} %get-tuple-element.23.refs_2_), channel_id=1, source_target_pairs={{0,1},{1,0},{2,3},{3,2},{4,5},{5,4},{6,7},{7,6},{8,9},{9,8},{10,11... | collective-permute-start | bytes 1376264 | tf_op jit(solution)/shard_map/ppermute | solution.py:355
  8.5 4.3 %collective-permute-done.8.refs_2_ = bf16[448,512]{1,0:T(8,128)(2,1)} collective-permute-done((bf16[448,512]{1,0:T(8,128)(2,1)S(1)}, bf16[448,512]{1,0:T(8,128)(2,1)}, u32[]{:S(2)}, u32[]{:S(2)}) %collective-permute-start.8) | collective-permute-done | bytes 458784 | tf_op jit(solution)/shard_map/ppermute | solution.py:355
  12.7 7.1 %collective-permute-start.9 = (bf16[448,512]{1,0:T(8,128)(2,1)}, bf16[448,512]{1,0:T(8,128)(2,1)}, u32[]{:S(2)}, u32[]{:S(2)}) collective-permute-start(bf16[448,512]{1,0:T(8,128)(2,1)} %collective-permute-done.8.refs_2_), channel_id=1, source_target_pairs={{0,1},{1,0},{2,3},{3,2},{4,5},{5,4},{6,7},{7,6},{8,9},{9,8},{10,11... | collective-permute-start | bytes 1376264 | tf_op jit(solution)/shard_map/ppermute | solution.py:355
  19.8 0.0 collective-permute-done.7.refs_1_
  19.8 0.0 copy-start.3
  19.8 0.8 copy-done.3
  20.6 0.0 collective-permute-start.10
  20.6 0.0 collective-permute-done.12.refs_2_
  20.6 0.0 collective-permute-start.3
  20.6 3.2 %collective-permute-done.refs_0_ = bf16[448,512]{1,0:T(8,128)(2,1)S(1)} collective-permute-done((bf16[448,512]{1,0:T(8,128)(2,1)S(1)}, bf16[448,512]{1,0:T(8,128)(2,1)S(1)}, u32[]{:S(2)}, u32[]{:S(2)}) %collective-permute-start) | collective-permute-done | bytes 458784 | tf_op jit(solution)/shard_map/ppermute | solution.py:355
  23.9 0.0 collective-permute-start.4
  23.9 0.0 collective-permute-done.2.refs_3_
  23.9 1.0 %collective-permute-start.1 = (bf16[448,512]{1,0:T(8,128)(2,1)S(1)}, bf16[448,512]{1,0:T(8,128)(2,1)}, u32[]{:S(2)}, u32[]{:S(2)}) collective-permute-start(bf16[448,512]{1,0:T(8,128)(2,1)S(1)} %collective-permute-done.refs_0_), channel_id=1, source_target_pairs={{0,1},{1,0},{2,3},{3,2},{4,5},{5,4},{6,7},{7,6},{8,9},{9,8},{10,11... | collective-permute-start | bytes 1376264 | tf_op jit(solution)/shard_map/ppermute | solution.py:355
  24.8 0.1 pad_add_fusion.where_ref
  24.9 0.0 collective-permute-done.9.refs_3_
  24.9 0.0 collective-permute-start.13
  24.9 7.8 %collective-permute-done.10.refs_0_ = bf16[448,512]{1,0:T(8,128)(2,1)S(1)} collective-permute-done((bf16[448,512]{1,0:T(8,128)(2,1)}, bf16[448,512]{1,0:T(8,128)(2,1)S(1)}, u32[]{:S(2)}, u32[]{:S(2)}) %collective-permute-start.10) | collective-permute-done | bytes 458784 | tf_op jit(solution)/shard_map/ppermute | solution.py:355
  32.7 0.2 collective-permute-start.11
  32.9 0.0 copy-start
  32.9 3.0 %copy-done = bf16[3584,1000]{0,1:T(8,128)(2,1)S(1)} copy-done((bf16[3584,1000]{0,1:T(8,128)(2,1)S(1)}, bf16[3584,1000]{0,1:T(8,128)(2,1)}, u32[]{:S(2)}) %copy-start) | copy-done | bytes 7168024
  35.9 0.0 copy-start.5
  35.9 0.7 copy-done.5
  36.6 0.0 copy-start.4
  36.6 2.4 %prepare.1.weight_ref = bf16[1000,4480]{1,0:T(8,128)(2,1)S(1)} custom-call(s32[3]{0:T(128)S(1)} %pad_add_fusion.where_ref, bf16[1000,3584]{1,0:T(8,128)(2,1)S(1)} %bitcast.14, f32[28,128]{1,0:T(8,128)S(1)} %bitcast.17), custom_call_target="tpu_custom_call" | custom-call | flops 1792000000 | bytes 14336000 | tf_op jit(solution)/shard_map/prepare/pallas_call | solution.py:58
  39.1 0.0 copy-done.4
  39.1 3.2 %near.3 = (f32[1000,512]{1,0:T(8,128)S(1)}, f32[16,512]{1,0:T(8,128)S(1)}) custom-call(s32[3]{0:T(128)S(1)} %pad_add_fusion.where_ref, bf16[1000,4480]{1,0:T(8,128)(2,1)S(1)} %prepare.1.weight_ref, bf16[448,512]{1,0:T(8,128)(2,1)S(1)} %get-tuple-element.22.refs_0_, bf16[448,512]{1,0:T(8,128)(2,1)S(1)} %copy-done.4, ...), custom_call_target="tpu_custom_call" | custom-call | flops 1835008000 | bytes 5419008 | tf_op jit(solution)/shard_map/near/pallas_call | solution.py:163
  42.3 0.0 collective-permute-done.3.refs_0_
  42.3 0.4 collective-permute-start.5
  42.8 0.0 collective-permute-done.4.refs_1_
  42.8 0.3 collective-permute-start.6
  43.1 0.0 collective-permute-done.1.refs_1_
  43.1 3.1 %near.2 = (f32[1000,512]{1,0:T(8,128)S(1)}, f32[16,512]{1,0:T(8,128)S(1)}) custom-call(s32[3]{0:T(128)S(1)} %pad_add_fusion.where_ref, bf16[1000,4480]{1,0:T(8,128)(2,1)S(1)} %prepare.1.weight_ref, bf16[448,512]{1,0:T(8,128)(2,1)S(1)} %collective-permute-done.refs_0_, bf16[448,512]{1,0:T(8,128)(2,1)} %collective-permute-done.1.refs_1_, ...), custom_call_target="tpu_custom_call" | custom-call | flops 1835008000 | bytes 5419008 | tf_op jit(solution)/shard_map/near/pallas_call | solution.py:163
  46.1 0.0 copy-start.1
  46.2 0.0 copy-start.2
  46.2 2.4 %middle.1 = (f32[1000,512]{1,0:T(8,128)S(1)}, f32[16,512]{1,0:T(8,128)S(1)}) custom-call(s32[3]{0:T(128)S(1)} %pad_add_fusion.where_ref, bf16[1000,4480]{1,0:T(8,128)(2,1)S(1)} %prepare.1.weight_ref, f32[1000,512]{1,0:T(8,128)S(1)} %get-tuple-element.12.near_ref, f32[16,512]{1,0:T(8,128)S(1)} %get-tuple-element.13.near_squares_ref, ...), custom_call_target="tpu_custom_call" | custom-call | flops 917504000 | bytes 6805504 | tf_op jit(solution)/shard_map/middle/pallas_call | solution.py:137
  48.5 0.0 collective-permute-done.13.refs_3_
  48.6 0.0 collective-permute-done.11.refs_1_
  48.6 0.0 copy-done.1
  48.6 0.0 copy-done.2
  48.6 3.3 %far.2 = (f32[8,128]{1,0:T(8,128)S(1)}, f32[8,128]{1,0:T(8,128)S(1)}) custom-call(s32[3]{0:T(128)S(1)} %pad_add_fusion.where_ref, bf16[1000,4480]{1,0:T(8,128)(2,1)S(1)} %prepare.1.weight_ref, f32[1000,512]{1,0:T(8,128)S(1)} %get-tuple-element.16.near_ref, f32[16,512]{1,0:T(8,128)S(1)} %get-tuple-element.17.squares_ref, s32[1024,128]{1,0:T(8,128)S(1)} %copy-done.1, ...), custom_call_target="tpu_custom_call" | custom-call | flops 3670016000 | bytes 9515008 | tf_op jit(solution)/shard_map/far/pallas_call | solution.py:260
  51.9 0.0 collective-permute-done.5.refs_0_
  51.9 0.0 collective-permute-done.6.refs_1_
  52.0 0.0 copy-start.6
  52.0 0.0 copy-start.7
  52.0 2.6 %far.3 = f32[8,16,128]{2,1,0:T(8,128)S(1)} custom-call(s32[3]{0:T(128)S(1)} %pad_add_fusion.where_ref, bf16[1000,4480]{1,0:T(8,128)(2,1)S(1)} %prepare.1.weight_ref, f32[1000,512]{1,0:T(8,128)S(1)} %get-tuple-element.14.near_ref, f32[16,512]{1,0:T(8,128)S(1)} %get-tuple-element.15.squares_ref, s32[1024,128]{1,0:T(8,128)S(1)} %copy-done.1, ...), custom_call_target="tpu_custom_call" | custom-call | flops 1835008000 | bytes 6805504 | tf_op jit(solution)/shard_map/far/pallas_call | solution.py:260
  54.6 7.5 %all_to_all.16.came_ref = f32[8,16,128]{2,1,0:T(8,128)S(1)} all-to-all(f32[8,16,128]{2,1,0:T(8,128)S(1)} %far.3), channel_id=1, replica_groups=mesh['seq'=32,'vocab'=8] {'vocab'}, dimensions={0} | all-to-all | bytes 131072 | tf_op jit(solution)/shard_map/all_to_all | solution.py:386
  62.1 0.0 copy-done.6
  62.1 0.0 copy-done.7
  62.1 0.8 losses.1
  62.9 0.1 copy.9
  62.9 16.9 %all_to_all.17 = f32[32,1,512]{2,1,0:T(1,128)S(1)} all-to-all(f32[32,1,512]{2,1,0:T(1,128)S(1)} %copy.9), channel_id=1, replica_groups=mesh['seq'=32,'vocab'=8] {'seq'}, dimensions={0} | all-to-all | bytes 131072 | tf_op jit(solution)/shard_map/all_to_all | solution.py:388
  79.9 0.6 finish.1
  (1 shorter events, 0.0 us)
Async XLA Ops:
  1.9 10.9 %collective-permute-start.8 = (bf16[448,512]{1,0:T(8,128)(2,1)S(1)}, bf16[448,512]{1,0:T(8,128)(2,1)}, u32[]{:S(2)}, u32[]{:S(2)}) collective-permute-start(bf16[448,512]{1,0:T(8,128)(2,1)S(1)} %get-tuple-element.22.refs_0_), channel_id=1, source_target_pairs={{0,2},{1,7},{2,4},{3,1},{4,6},{5,3},{6,0},{7,5},{8,10},{9,15},{10,... | collective-permute-start | bytes 1376264 | tf_op jit(solution)/shard_map/ppermute | solution.py:355
  5.5 14.4 %collective-permute-start.7 = (bf16[448,512]{1,0:T(8,128)(2,1)S(1)}, bf16[448,512]{1,0:T(8,128)(2,1)S(1)}, u32[]{:S(2)}, u32[]{:S(2)}) collective-permute-start(bf16[448,512]{1,0:T(8,128)(2,1)S(1)} %get-tuple-element.22.refs_0_), channel_id=1, source_target_pairs={{0,1},{1,0},{2,3},{3,2},{4,5},{5,4},{6,7},{7,6},{8,9},{9,8},{10,11... | collective-permute-start | bytes 1376264 | tf_op jit(solution)/shard_map/ppermute | solution.py:355
  5.5 15.1 %collective-permute-start.12 = (bf16[448,512]{1,0:T(8,128)(2,1)S(1)}, bf16[448,512]{1,0:T(8,128)(2,1)S(1)}, u32[]{:S(2)}, u32[]{:S(2)}) collective-permute-start(bf16[448,512]{1,0:T(8,128)(2,1)S(1)} %get-tuple-element.22.refs_0_), channel_id=1, source_target_pairs={{0,6},{1,3},{2,0},{3,5},{4,2},{5,7},{6,4},{7,1},{8,14},{9,11},{10,... | collective-permute-start | bytes 1376264 | tf_op jit(solution)/shard_map/ppermute | solution.py:355
  6.3 17.6 %collective-permute-start = (bf16[448,512]{1,0:T(8,128)(2,1)S(1)}, bf16[448,512]{1,0:T(8,128)(2,1)S(1)}, u32[]{:S(2)}, u32[]{:S(2)}) collective-permute-start(bf16[448,512]{1,0:T(8,128)(2,1)S(1)} %get-tuple-element.23.refs_2_), channel_id=1, source_target_pairs={{0,6},{1,3},{2,0},{3,5},{4,2},{5,7},{6,4},{7,1},{8,14},{9,11},{10,... | collective-permute-start | bytes 1376264 | tf_op jit(solution)/shard_map/ppermute | solution.py:355
  7.3 16.6 %collective-permute-start.2 = (bf16[448,512]{1,0:T(8,128)(2,1)S(1)}, bf16[448,512]{1,0:T(8,128)(2,1)S(1)}, u32[]{:S(2)}, u32[]{:S(2)}) collective-permute-start(bf16[448,512]{1,0:T(8,128)(2,1)S(1)} %get-tuple-element.23.refs_2_), channel_id=1, source_target_pairs={{0,1},{1,0},{2,3},{3,2},{4,5},{5,4},{6,7},{7,6},{8,9},{9,8},{10,11... | collective-permute-start | bytes 1376264 | tf_op jit(solution)/shard_map/ppermute | solution.py:355
  12.7 12.2 %collective-permute-start.9 = (bf16[448,512]{1,0:T(8,128)(2,1)}, bf16[448,512]{1,0:T(8,128)(2,1)}, u32[]{:S(2)}, u32[]{:S(2)}) collective-permute-start(bf16[448,512]{1,0:T(8,128)(2,1)} %collective-permute-done.8.refs_2_), channel_id=1, source_target_pairs={{0,1},{1,0},{2,3},{3,2},{4,5},{5,4},{6,7},{7,6},{8,9},{9,8},{10,11... | collective-permute-start | bytes 1376264 | tf_op jit(solution)/shard_map/ppermute | solution.py:355
  19.8 0.8 copy-start.3
  20.6 12.1 %collective-permute-start.10 = (bf16[448,512]{1,0:T(8,128)(2,1)}, bf16[448,512]{1,0:T(8,128)(2,1)S(1)}, u32[]{:S(2)}, u32[]{:S(2)}) collective-permute-start(bf16[448,512]{1,0:T(8,128)(2,1)} %collective-permute-done.8.refs_2_), channel_id=1, source_target_pairs={{0,2},{1,7},{2,4},{3,1},{4,6},{5,3},{6,0},{7,5},{8,10},{9,15},{10,... | collective-permute-start | bytes 1376264 | tf_op jit(solution)/shard_map/ppermute | solution.py:355
  20.6 21.7 %collective-permute-start.3 = (bf16[448,512]{1,0:T(8,128)(2,1)S(1)}, bf16[448,512]{1,0:T(8,128)(2,1)S(1)}, u32[]{:S(2)}, u32[]{:S(2)}) collective-permute-start(bf16[448,512]{1,0:T(8,128)(2,1)S(1)} %get-tuple-element.23.refs_2_), channel_id=1, source_target_pairs={{0,2},{1,7},{2,4},{3,1},{4,6},{5,3},{6,0},{7,5},{8,10},{9,15},{10,... | collective-permute-start | bytes 1376264 | tf_op jit(solution)/shard_map/ppermute | solution.py:355
  23.9 18.9 %collective-permute-start.4 = (bf16[448,512]{1,0:T(8,128)(2,1)S(1)}, bf16[448,512]{1,0:T(8,128)(2,1)}, u32[]{:S(2)}, u32[]{:S(2)}) collective-permute-start(bf16[448,512]{1,0:T(8,128)(2,1)S(1)} %collective-permute-done.refs_0_), channel_id=1, source_target_pairs={{0,6},{1,3},{2,0},{3,5},{4,2},{5,7},{6,4},{7,1},{8,14},{9,11},{10,... | collective-permute-start | bytes 1376264 | tf_op jit(solution)/shard_map/ppermute | solution.py:355
  23.9 19.2 %collective-permute-start.1 = (bf16[448,512]{1,0:T(8,128)(2,1)S(1)}, bf16[448,512]{1,0:T(8,128)(2,1)}, u32[]{:S(2)}, u32[]{:S(2)}) collective-permute-start(bf16[448,512]{1,0:T(8,128)(2,1)S(1)} %collective-permute-done.refs_0_), channel_id=1, source_target_pairs={{0,1},{1,0},{2,3},{3,2},{4,5},{5,4},{6,7},{7,6},{8,9},{9,8},{10,11... | collective-permute-start | bytes 1376264 | tf_op jit(solution)/shard_map/ppermute | solution.py:355
  24.9 23.6 %collective-permute-start.13 = (bf16[448,512]{1,0:T(8,128)(2,1)S(1)}, bf16[448,512]{1,0:T(8,128)(2,1)S(1)}, u32[]{:S(2)}, u32[]{:S(2)}) collective-permute-start(bf16[448,512]{1,0:T(8,128)(2,1)S(1)} %collective-permute-done.12.refs_2_), channel_id=1, source_target_pairs={{0,1},{1,0},{2,3},{3,2},{4,5},{5,4},{6,7},{7,6},{8,9},{9,8},{10,11... | collective-permute-start | bytes 1376264 | tf_op jit(solution)/shard_map/ppermute | solution.py:355
  32.7 15.9 %collective-permute-start.11 = (bf16[448,512]{1,0:T(8,128)(2,1)S(1)}, bf16[448,512]{1,0:T(8,128)(2,1)S(1)}, u32[]{:S(2)}, u32[]{:S(2)}) collective-permute-start(bf16[448,512]{1,0:T(8,128)(2,1)S(1)} %collective-permute-done.10.refs_0_), channel_id=1, source_target_pairs={{0,1},{1,0},{2,3},{3,2},{4,5},{5,4},{6,7},{7,6},{8,9},{9,8},{10,11... | collective-permute-start | bytes 1376264 | tf_op jit(solution)/shard_map/ppermute | solution.py:355
  32.9 3.1 %copy-start = (bf16[3584,1000]{0,1:T(8,128)(2,1)S(1)}, bf16[3584,1000]{0,1:T(8,128)(2,1)}, u32[]{:S(2)}) copy-start(bf16[3584,1000]{0,1:T(8,128)(2,1)} %param.9) | copy-start | bytes 21504004
  35.9 0.7 copy-start.5
  36.6 2.4 %copy-start.4 = (bf16[448,512]{1,0:T(8,128)(2,1)S(1)}, bf16[448,512]{1,0:T(8,128)(2,1)}, u32[]{:S(2)}) copy-start(bf16[448,512]{1,0:T(8,128)(2,1)} %copy-done.3) | copy-start | bytes 1376260
  42.3 9.6 %collective-permute-start.5 = (bf16[448,512]{1,0:T(8,128)(2,1)S(1)}, bf16[448,512]{1,0:T(8,128)(2,1)S(1)}, u32[]{:S(2)}, u32[]{:S(2)}) collective-permute-start(bf16[448,512]{1,0:T(8,128)(2,1)S(1)} %collective-permute-done.3.refs_0_), channel_id=1, source_target_pairs={{0,1},{1,0},{2,3},{3,2},{4,5},{5,4},{6,7},{7,6},{8,9},{9,8},{10,11... | collective-permute-start | bytes 1376264 | tf_op jit(solution)/shard_map/ppermute | solution.py:355
  42.8 9.2 %collective-permute-start.6 = (bf16[448,512]{1,0:T(8,128)(2,1)}, bf16[448,512]{1,0:T(8,128)(2,1)S(1)}, u32[]{:S(2)}, u32[]{:S(2)}) collective-permute-start(bf16[448,512]{1,0:T(8,128)(2,1)} %collective-permute-done.4.refs_1_), channel_id=1, source_target_pairs={{0,1},{1,0},{2,3},{3,2},{4,5},{5,4},{6,7},{7,6},{8,9},{9,8},{10,11... | collective-permute-start | bytes 1376264 | tf_op jit(solution)/shard_map/ppermute | solution.py:355
  46.1 2.4 %copy-start.1 = (s32[1024,128]{1,0:T(8,128)S(1)}, s32[1024,128]{1,0:T(8,128)}, u32[]{:S(2)}) copy-start(s32[1024,128]{1,0:T(8,128)} %ids_ref.3) | copy-start | bytes 1572868
  46.2 2.4 %copy-start.2 = (f32[1024,128]{1,0:T(8,128)S(1)}, f32[1024,128]{1,0:T(8,128)}, u32[]{:S(2)}) copy-start(f32[1024,128]{1,0:T(8,128)} %probs_ref.3) | copy-start | bytes 1572868
  52.0 10.1 %copy-start.6 = (s32[1024]{0:T(1024)S(1)}, s32[1024]{0:T(1024)}, u32[]{:S(2)}) copy-start(s32[1024]{0:T(1024)} %param.12) | copy-start | bytes 12292
  52.0 10.1 %copy-start.7 = (s32[8,2]{0,1:T(2,128)S(1)}, s32[8,2]{0,1:T(2,128)}, u32[]{:S(2)}) copy-start(s32[8,2]{0,1:T(2,128)} %param.13) | copy-start | bytes 196
